TPU v7x, 32 devices: a whole 2x2x4 slice. The times are simulated.
32 devices in a mesh: sec: 8 (over z, x), chan: 4 (over y, core).
Axes of the slice: x: 2, y: 2, z: 4, core: 2. Of those that a mesh axis runs over, the one named last changes fastest.
Arguments:
- state_blocks: bfloat16 [8, 512, 512], P('sec'), may hold values from -6 to 6
- left_blocks: bfloat16 [32, 8, 512, 512], P('chan', 'sec'), may hold values from -0.25 to 0.25
- right_blocks: bfloat16 [32, 8, 512, 512], P('chan', 'sec'), may hold values from -0.25 to 0.25
- widths: int32 [8], P('sec'), may hold values from 128 to 512
- step_sizes: float32 [8], P('sec'), may hold values from 0.1 to 0.4
- shifts: int32 [32], P('chan'), may hold values from -1 to 1
Outputs:
- update: bfloat16 [8, 512, 512], P('sec', 'chan')
- new_left: bfloat16 [32, 8, 512, 512], P('chan', 'sec')
All inputs are finite; a program needn't handle non-finite values.
Results may differ from a plain program's by a relative error of at most 0.012.
Values may be sent and summed in bfloat16 or wider, within the bound.
No kernel may reach another device: no remote copies, remote signals or barrier semaphores. Data moves between devices by JAX's collectives and lax.ppermute only.
A program may use at most 64 MiB of HBM per device.

v0:
```python
import jax
import jax.numpy as jnp
from jax import lax
from jax.sharding import PartitionSpec as P

REACH = 1


def padded_2(shard, sides, width):
    for axis, dim in sides:
        count, length = (lax.axis_size(axis), shard.shape[dim])
        up = [(i, (i + 1) % count) for i in range(count - 1)]
        down = [(j, i) for i, j in up]
        last = lax.slice_in_dim(shard, length - width, length, axis=dim)
        initial = lax.slice_in_dim(shard, 0, width, axis=dim)
        before = lax.ppermute(last, axis, up)
        after = lax.ppermute(initial, axis, down)
        shard = jnp.concatenate([before, shard, after], axis=dim)
    return shard


def padded_term(left, right, source):
    halfway = jnp.dot(left, source, preferred_element_type=jnp.float32).astype(jnp.bfloat16)
    return lax.dot_general(
        halfway, right, (((1,), (1,)), ((), ())), preferred_element_type=jnp.float32
    )


def shards(state_blocks, left_blocks, right_blocks, widths, step_sizes, shifts):
    padded = state_blocks.shape[1]
    chan_count = left_blocks.shape[0]
    positions = jnp.arange(padded, dtype=jnp.int32)
    within = positions[None, :] < widths[:, None]
    inside = within[:, :, None] & within[:, None, :]
    states = jnp.where(inside, state_blocks, jnp.zeros_like(state_blocks))
    extended = padded_2(states, (("sec", 0),), REACH)
    sector = 0
    total = jnp.zeros((padded, padded), jnp.float32)
    for channel in range(chan_count):
        offset = shifts[channel]
        source = lax.dynamic_slice_in_dim(extended, sector + REACH - offset, 1, 0)[0]
        left = left_blocks[channel, sector]
        right = right_blocks[channel, sector]
        total = total + padded_term(left, right, source)
    sector_sums = [total]
    partial_sum = jnp.stack(sector_sums)
    share_rows = padded // lax.axis_size("chan")
    row_start = lax.axis_index("chan") * share_rows
    summed_rows = lax.psum_scatter(partial_sum, "chan", scatter_dimension=1, tiled=True)
    inside_rows = lax.dynamic_slice_in_dim(inside, row_start, share_rows, 1)
    state_rows = lax.dynamic_slice_in_dim(states, row_start, share_rows, 1)
    product_rows = jnp.where(inside_rows, summed_rows, jnp.zeros_like(summed_rows))
    corrected = state_rows.astype(jnp.float32) - step_sizes[:, None, None] * product_rows
    update_rows = jnp.where(inside_rows, corrected, jnp.zeros_like(corrected)).astype(jnp.bfloat16)
    update = lax.all_gather(update_rows, "chan", axis=1, tiled=True)
    update_ext = padded_2(update, (("sec", 0),), REACH)
    norm_factor = padded ** (-0.5)
    channel_rows = []
    for channel in range(chan_count):
        offset = shifts[channel]
        sector = 0
        ket_block = lax.dynamic_slice_in_dim(update_ext, sector + REACH - offset, 1, 0)[0]
        pulled = jnp.dot(
            left_blocks[channel, sector], ket_block, preferred_element_type=jnp.float32
        ).astype(jnp.bfloat16)
        rotated = lax.dot_general(
            update[sector], pulled, (((0,), (0,)), ((), ())), preferred_element_type=jnp.float32
        )
        rotated_list = [(rotated * norm_factor).astype(jnp.bfloat16)]
        channel_rows.append(jnp.stack(rotated_list))
    new_left = jnp.stack(channel_rows)
    return (update_rows, new_left)


def solution(mesh):
    placed = (
        P("sec", None, None),
        P("chan", "sec", None, None),
        P("chan", "sec", None, None),
        P("sec"),
        P("sec"),
        P("chan"),
    )
    return jax.shard_map(
        shards,
        mesh=mesh,
        in_specs=placed,
        out_specs=(P("sec", "chan", None), P("chan", "sec", None, None)),
        check_vma=False,
    )
```

profile of v0, /device:TPU:9, one launch (start us, length us, event | category | flops | bytes accessed | tf_op | source)
XLA Modules:
  0.0 149.3 jit_solution(9315964518778124198)
XLA Ops:
  7.2 0.0 reduce-scatter.2.cloned.1.call-start
  7.9 1.3 broadcast_select_fusion
  9.1 3.0 %collective-permute-start.1 = (bf16[1,512,512]{2,1,0:T(8,128)(2,1)S(1)}, bf16[1,512,512]{2,1,0:T(8,128)(2,1)S(1)}, u32[]{:S(2)}, u32[]{:S(2)}) collective-permute-start(bf16[1,512,512]{2,1,0:T(8,128)(2,1)S(1)} %broadcast_select_fusion), channel_id=1, source_target_pairs={{4,0},{8,4},{12,8},{16,12},{20,16},{24,20},{28,24},{5,1},{9,5},{13... | collective-permute-start | bytes 1572872 | tf_op jit(solution)/shard_map/ppermute | solution.py:17
  12.1 2.3 %collective-permute-start = (bf16[1,512,512]{2,1,0:T(8,128)(2,1)S(1)}, bf16[1,512,512]{2,1,0:T(8,128)(2,1)S(1)}, u32[]{:S(2)}, u32[]{:S(2)}) collective-permute-start(bf16[1,512,512]{2,1,0:T(8,128)(2,1)S(1)} %broadcast_select_fusion), channel_id=1, source_target_pairs={{0,4},{4,8},{8,12},{12,16},{16,20},{20,24},{24,28},{1,5},{5,9},{9,... | collective-permute-start | bytes 1572872 | tf_op jit(solution)/shard_map/ppermute | solution.py:16
  14.4 1.6 %fusion.210 = (s32[1]{0:T(128)}, s32[1]{0:T(128)}, s32[1]{0:T(128)}, s32[1]{0:T(128)}, s32[1]{0:T(128)}, /*index=5*/s32[1]{0:T(128)}, s32[1]{0:T(128)}, s32[1]{0:T(128)}) fusion(s32[8]{0:T(128)} %param.11), kind=kLoop, calls=%fused_computation.169 | loop fusion | bytes 64 | tf_op jit(solution)/shard_map/slice | solution.py:40
  26.2 8.9 %collective-permute-done.1 = bf16[1,512,512]{2,1,0:T(8,128)(2,1)S(1)} collective-permute-done((bf16[1,512,512]{2,1,0:T(8,128)(2,1)S(1)}, bf16[1,512,512]{2,1,0:T(8,128)(2,1)S(1)}, u32[]{:S(2)}, u32[]{:S(2)}) %collective-permute-start.1) | collective-permute-done | bytes 524320 | tf_op jit(solution)/shard_map/ppermute | solution.py:17
  35.1 0.9 collective-permute-done
  36.0 0.2 pad_maximum_fusion
  36.2 3.0 %fusion.25 = f32[512,512]{1,0:T(8,128)} fusion(bf16[8,1,512,512]{3,2,1,0:T(8,128)(2,1)} %param.8, bf16[3,512,512]{2,1,0:T(8,128)(2,1)S(1)} %pad_maximum_fusion, s32[]{:T(128)S(6)} %select_n.49, bf16[8,1,512,512]{3,2,1,0:T(8,128)(2,1)} %param.7), kind=kOutput, calls=%fused_computation.57 | convolution fusion | flops 537133056 | bytes 2621444 | tf_op jit(solution)/shard_map/dot_general | solution.py:24
  39.2 2.4 %convolution_add_fusion.6 = f32[512,512]{1,0:T(8,128)S(1)} fusion(f32[512,512]{1,0:T(8,128)} %fusion.25, bf16[8,1,512,512]{3,2,1,0:T(8,128)(2,1)} %param.8, bf16[3,512,512]{2,1,0:T(8,128)(2,1)S(1)} %pad_maximum_fusion, s32[]{:T(128)S(6)} %select_n.50, bf16[8,1,512,512]{3,2,1,0:T(8,128)(2,1)} %param.7), kind=kOutput, calls=%fused_computation.16 | convolution fusion | flops 537395200 | bytes 3670020 | tf_op jit(solution)/shard_map/dot_general | solution.py:24
  41.7 3.0 %convolution_add_fusion.5 = f32[512,512]{1,0:T(8,128)} fusion(f32[512,512]{1,0:T(8,128)S(1)} %convolution_add_fusion.6, bf16[8,1,512,512]{3,2,1,0:T(8,128)(2,1)} %param.8, bf16[3,512,512]{2,1,0:T(8,128)(2,1)S(1)} %pad_maximum_fusion, s32[]{:T(128)S(6)} %select_n.51, bf16[8,1,512,512]{3,2,1,0:T(8,128)(2,1)} %param.7), kind=kOutput, calls=%fused_computation.15 | convolution fusion | flops 537395200 | bytes 3670020 | tf_op jit(solution)/shard_map/dot_general | solution.py:24
  44.7 2.4 %convolution_add_fusion.4 = f32[512,512]{1,0:T(8,128)S(1)} fusion(f32[512,512]{1,0:T(8,128)} %convolution_add_fusion.5, bf16[8,1,512,512]{3,2,1,0:T(8,128)(2,1)} %param.8, bf16[3,512,512]{2,1,0:T(8,128)(2,1)S(1)} %pad_maximum_fusion, s32[]{:T(128)S(6)} %select_n.52, bf16[8,1,512,512]{3,2,1,0:T(8,128)(2,1)} %param.7), kind=kOutput, calls=%fused_computation.14 | convolution fusion | flops 537395200 | bytes 3670020 | tf_op jit(solution)/shard_map/dot_general | solution.py:24
  47.1 3.0 %convolution_add_fusion.3 = f32[512,512]{1,0:T(8,128)} fusion(f32[512,512]{1,0:T(8,128)S(1)} %convolution_add_fusion.4, bf16[8,1,512,512]{3,2,1,0:T(8,128)(2,1)} %param.8, bf16[3,512,512]{2,1,0:T(8,128)(2,1)S(1)} %pad_maximum_fusion, s32[]{:T(128)S(6)} %select_n.53, bf16[8,1,512,512]{3,2,1,0:T(8,128)(2,1)} %param.7), kind=kOutput, calls=%fused_computation.13 | convolution fusion | flops 537395200 | bytes 3670020 | tf_op jit(solution)/shard_map/dot_general | solution.py:24
  50.2 3.4 %convolution_add_fusion.2 = f32[512,512]{1,0:T(8,128)} fusion(f32[512,512]{1,0:T(8,128)} %convolution_add_fusion.3, bf16[8,1,512,512]{3,2,1,0:T(8,128)(2,1)} %param.8, bf16[3,512,512]{2,1,0:T(8,128)(2,1)S(1)} %pad_maximum_fusion, s32[]{:T(128)S(6)} %select_n.54, bf16[8,1,512,512]{3,2,1,0:T(8,128)(2,1)} %param.7), kind=kOutput, calls=%fused_computation.12 | convolution fusion | flops 537395200 | bytes 3670020 | tf_op jit(solution)/shard_map/dot_general | solution.py:24
  53.6 2.4 %convolution_add_fusion.1 = f32[512,512]{1,0:T(8,128)S(1)} fusion(f32[512,512]{1,0:T(8,128)} %convolution_add_fusion.2, bf16[8,1,512,512]{3,2,1,0:T(8,128)(2,1)} %param.8, bf16[3,512,512]{2,1,0:T(8,128)(2,1)S(1)} %pad_maximum_fusion, s32[]{:T(128)S(6)} %select_n.55, bf16[8,1,512,512]{3,2,1,0:T(8,128)(2,1)} %param.7), kind=kOutput, calls=%fused_computation.11 | convolution fusion | flops 537395200 | bytes 3670020 | tf_op jit(solution)/shard_map/dot_general | solution.py:24
  56.0 3.0 %fusion = f32[1,512,512]{2,1,0:T(8,128)} fusion(f32[512,512]{1,0:T(8,128)S(1)} %convolution_add_fusion.1, bf16[8,1,512,512]{3,2,1,0:T(8,128)(2,1)} %param.8, bf16[3,512,512]{2,1,0:T(8,128)(2,1)S(1)} %pad_maximum_fusion, s32[]{:T(128)S(6)} %select_n.56, bf16[8,1,512,512]{3,2,1,0:T(8,128)(2,1)} %param.7), kind=kOutput, calls=%fused_computation.10 | convolution fusion | flops 537395200 | bytes 3670020 | tf_op jit(solution)/shard_map/dot_general | solution.py:24
  59.7 0.2 broadcast_and_fusion
  59.9 24.9 %reduce-scatter.2.cloned.1.call-done = f32[1,128,512]{2,1,0:T(8,128)} async-done(((f32[1,512,512]{2,1,0:T(8,128)}), f32[1,128,512]{2,1,0:T(8,128)}) %reduce-scatter.2.cloned.1.call-update) | async-done | bytes 262160 | tf_op jit(solution)/shard_map/reduce_scatter | solution.py:49
  84.8 1.0 select_convert_fusion
  85.8 7.3 %all_gather.3 = bf16[1,512,512]{2,1,0:T(8,128)(2,1)S(1)} all-gather(bf16[1,128,512]{2,1,0:T(8,128)(2,1)S(1)} %select_convert_fusion), channel_id=1, replica_groups=mesh['sec'=8,'chan'=4] {'chan'}, dimensions={1}, use_global_device_ids=true | all-gather | bytes 655360 | tf_op jit(solution)/shard_map/all_gather | solution.py:55
  93.1 3.1 %collective-permute-start.2 = (bf16[1,512,512]{2,1,0:T(8,128)(2,1)S(1)}, bf16[1,512,512]{2,1,0:T(8,128)(2,1)S(1)}, u32[]{:S(2)}, u32[]{:S(2)}) collective-permute-start(bf16[1,512,512]{2,1,0:T(8,128)(2,1)S(1)} %all_gather.3), channel_id=1, source_target_pairs={{0,4},{4,8},{8,12},{12,16},{16,20},{20,24},{24,28},{1,5},{5,9},{9,... | collective-permute-start | bytes 1572872 | tf_op jit(solution)/shard_map/ppermute | solution.py:16
  96.2 3.3 %collective-permute-start.3 = (bf16[1,512,512]{2,1,0:T(8,128)(2,1)S(1)}, bf16[1,512,512]{2,1,0:T(8,128)(2,1)S(1)}, u32[]{:S(2)}, u32[]{:S(2)}) collective-permute-start(bf16[1,512,512]{2,1,0:T(8,128)(2,1)S(1)} %all_gather.3), channel_id=1, source_target_pairs={{4,0},{8,4},{12,8},{16,12},{20,16},{24,20},{28,24},{5,1},{9,5},{13... | collective-permute-start | bytes 1572872 | tf_op jit(solution)/shard_map/ppermute | solution.py:17
  99.5 19.1 %collective-permute-done.2 = bf16[1,512,512]{2,1,0:T(8,128)(2,1)S(1)} collective-permute-done((bf16[1,512,512]{2,1,0:T(8,128)(2,1)S(1)}, bf16[1,512,512]{2,1,0:T(8,128)(2,1)S(1)}, u32[]{:S(2)}, u32[]{:S(2)}) %collective-permute-start.2) | collective-permute-done | bytes 524320 | tf_op jit(solution)/shard_map/ppermute | solution.py:16
  118.6 2.4 %collective-permute-done.3 = bf16[1,512,512]{2,1,0:T(8,128)(2,1)S(1)} collective-permute-done((bf16[1,512,512]{2,1,0:T(8,128)(2,1)S(1)}, bf16[1,512,512]{2,1,0:T(8,128)(2,1)S(1)}, u32[]{:S(2)}, u32[]{:S(2)}) %collective-permute-start.3) | collective-permute-done | bytes 524320 | tf_op jit(solution)/shard_map/ppermute | solution.py:17
  121.0 2.7 %fusion.24 = bf16[8,1,512,512]{3,2,1,0:T(8,128)(2,1)} fusion(bf16[1,512,512]{2,1,0:T(8,128)(2,1)S(1)} %all_gather.3, bf16[3,512,512]{2,1,0:T(8,128)(2,1)S(1)} %constant_dynamic-update-slice_fusion, s32[]{:T(128)S(6)} %select_n.49, bf16[8,1,512,512]{3,2,1,0:T(8,128)(2,1)} %param.7), kind=kOutput, calls=%fused_computation.56 | convolution fusion | flops 537657344 | bytes 2097156 | tf_op jit(solution)/shard_map/dot_general | solution.py:66
  123.7 2.7 %fusion.22 = bf16[8,1,512,512]{3,2,1,0:T(8,128)(2,1)} fusion(bf16[8,1,512,512]{3,2,1,0:T(8,128)(2,1)} %fusion.24, bf16[1,512,512]{2,1,0:T(8,128)(2,1)S(1)} %all_gather.3, bf16[3,512,512]{2,1,0:T(8,128)(2,1)S(1)} %constant_dynamic-update-slice_fusion, s32[]{:T(128)S(6)} %select_n.50, bf16[8,1,512,512]{3,2,1,0:T(8,128)(2,1)} %param.7), kind=kOutput, calls=%fused_computation.54 | convolution fusion | flops 537657344 | bytes 2097156 | tf_op jit(solution)/shard_map/dot_general | solution.py:66
  126.4 2.7 %fusion.20 = bf16[8,1,512,512]{3,2,1,0:T(8,128)(2,1)} fusion(bf16[8,1,512,512]{3,2,1,0:T(8,128)(2,1)} %fusion.22, bf16[1,512,512]{2,1,0:T(8,128)(2,1)S(1)} %all_gather.3, bf16[3,512,512]{2,1,0:T(8,128)(2,1)S(1)} %constant_dynamic-update-slice_fusion, s32[]{:T(128)S(6)} %select_n.51, bf16[8,1,512,512]{3,2,1,0:T(8,128)(2,1)} %param.7), kind=kOutput, calls=%fused_computation.52 | convolution fusion | flops 537657344 | bytes 2097156 | tf_op jit(solution)/shard_map/dot_general | solution.py:66
  129.1 2.7 %fusion.18 = bf16[8,1,512,512]{3,2,1,0:T(8,128)(2,1)} fusion(bf16[8,1,512,512]{3,2,1,0:T(8,128)(2,1)} %fusion.20, bf16[1,512,512]{2,1,0:T(8,128)(2,1)S(1)} %all_gather.3, bf16[3,512,512]{2,1,0:T(8,128)(2,1)S(1)} %constant_dynamic-update-slice_fusion, s32[]{:T(128)S(6)} %select_n.52, bf16[8,1,512,512]{3,2,1,0:T(8,128)(2,1)} %param.7), kind=kOutput, calls=%fused_computation.50 | convolution fusion | flops 537657344 | bytes 2097156 | tf_op jit(solution)/shard_map/dot_general | solution.py:66
  131.8 2.7 %fusion.16 = bf16[8,1,512,512]{3,2,1,0:T(8,128)(2,1)} fusion(bf16[8,1,512,512]{3,2,1,0:T(8,128)(2,1)} %fusion.18, bf16[1,512,512]{2,1,0:T(8,128)(2,1)S(1)} %all_gather.3, bf16[3,512,512]{2,1,0:T(8,128)(2,1)S(1)} %constant_dynamic-update-slice_fusion, s32[]{:T(128)S(6)} %select_n.53, bf16[8,1,512,512]{3,2,1,0:T(8,128)(2,1)} %param.7), kind=kOutput, calls=%fused_computation.48 | convolution fusion | flops 537657344 | bytes 2097156 | tf_op jit(solution)/shard_map/dot_general | solution.py:66
  134.4 2.7 %fusion.14 = bf16[8,1,512,512]{3,2,1,0:T(8,128)(2,1)} fusion(bf16[8,1,512,512]{3,2,1,0:T(8,128)(2,1)} %fusion.16, bf16[1,512,512]{2,1,0:T(8,128)(2,1)S(1)} %all_gather.3, bf16[3,512,512]{2,1,0:T(8,128)(2,1)S(1)} %constant_dynamic-update-slice_fusion, s32[]{:T(128)S(6)} %select_n.54, bf16[8,1,512,512]{3,2,1,0:T(8,128)(2,1)} %param.7), kind=kOutput, calls=%fused_computation.46 | convolution fusion | flops 537657344 | bytes 2097156 | tf_op jit(solution)/shard_map/dot_general | solution.py:66
  137.1 2.7 %fusion.12 = bf16[8,1,512,512]{3,2,1,0:T(8,128)(2,1)} fusion(bf16[8,1,512,512]{3,2,1,0:T(8,128)(2,1)} %fusion.14, bf16[1,512,512]{2,1,0:T(8,128)(2,1)S(1)} %all_gather.3, bf16[3,512,512]{2,1,0:T(8,128)(2,1)S(1)} %constant_dynamic-update-slice_fusion, s32[]{:T(128)S(6)} %select_n.55, bf16[8,1,512,512]{3,2,1,0:T(8,128)(2,1)} %param.7), kind=kOutput, calls=%fused_computation.44 | convolution fusion | flops 537657344 | bytes 2097156 | tf_op jit(solution)/shard_map/dot_general | solution.py:66
  139.8 2.7 %fusion.10 = bf16[8,1,512,512]{3,2,1,0:T(8,128)(2,1)} fusion(bf16[8,1,512,512]{3,2,1,0:T(8,128)(2,1)} %fusion.12, bf16[1,512,512]{2,1,0:T(8,128)(2,1)S(1)} %all_gather.3, bf16[3,512,512]{2,1,0:T(8,128)(2,1)S(1)} %constant_dynamic-update-slice_fusion, s32[]{:T(128)S(6)} %select_n.56, bf16[8,1,512,512]{3,2,1,0:T(8,128)(2,1)} %param.7), kind=kOutput, calls=%fused_computation.42 | convolution fusion | flops 537657344 | bytes 2097156 | tf_op jit(solution)/shard_map/dot_general | solution.py:66
  (7 shorter events, 0.1 us)
Async XLA Ops:
  7.2 77.6 %reduce-scatter.2.cloned.1.call-start = ((), (), s32[]{:S(2)}) async-start(), calls=%async_computation.1 | async-start | bytes 1310720 | tf_op jit(solution)/shard_map/reduce_scatter | solution.py:49
  9.1 25.9 %collective-permute-start.1 = (bf16[1,512,512]{2,1,0:T(8,128)(2,1)S(1)}, bf16[1,512,512]{2,1,0:T(8,128)(2,1)S(1)}, u32[]{:S(2)}, u32[]{:S(2)}) collective-permute-start(bf16[1,512,512]{2,1,0:T(8,128)(2,1)S(1)} %broadcast_select_fusion), channel_id=1, source_target_pairs={{4,0},{8,4},{12,8},{16,12},{20,16},{24,20},{28,24},{5,1},{9,5},{13... | collective-permute-start | bytes 1572872 | tf_op jit(solution)/shard_map/ppermute | solution.py:17
  12.1 23.9 %collective-permute-start = (bf16[1,512,512]{2,1,0:T(8,128)(2,1)S(1)}, bf16[1,512,512]{2,1,0:T(8,128)(2,1)S(1)}, u32[]{:S(2)}, u32[]{:S(2)}) collective-permute-start(bf16[1,512,512]{2,1,0:T(8,128)(2,1)S(1)} %broadcast_select_fusion), channel_id=1, source_target_pairs={{0,4},{4,8},{8,12},{12,16},{16,20},{20,24},{24,28},{1,5},{5,9},{9,... | collective-permute-start | bytes 1572872 | tf_op jit(solution)/shard_map/ppermute | solution.py:16
  85.8 40.6 %copy-start = (bf16[1,128,512]{2,1,0:T(8,128)(2,1)}, bf16[1,128,512]{2,1,0:T(8,128)(2,1)S(1)}, u32[]{:S(2)}) copy-start(bf16[1,128,512]{2,1,0:T(8,128)(2,1)S(1)} %select_convert_fusion) | copy-start | bytes 393220
  93.1 25.4 %collective-permute-start.2 = (bf16[1,512,512]{2,1,0:T(8,128)(2,1)S(1)}, bf16[1,512,512]{2,1,0:T(8,128)(2,1)S(1)}, u32[]{:S(2)}, u32[]{:S(2)}) collective-permute-start(bf16[1,512,512]{2,1,0:T(8,128)(2,1)S(1)} %all_gather.3), channel_id=1, source_target_pairs={{0,4},{4,8},{8,12},{12,16},{16,20},{20,24},{24,28},{1,5},{5,9},{9,... | collective-permute-start | bytes 1572872 | tf_op jit(solution)/shard_map/ppermute | solution.py:16
  96.2 24.8 %collective-permute-start.3 = (bf16[1,512,512]{2,1,0:T(8,128)(2,1)S(1)}, bf16[1,512,512]{2,1,0:T(8,128)(2,1)S(1)}, u32[]{:S(2)}, u32[]{:S(2)}) collective-permute-start(bf16[1,512,512]{2,1,0:T(8,128)(2,1)S(1)} %all_gather.3), channel_id=1, source_target_pairs={{4,0},{8,4},{12,8},{16,12},{20,16},{24,20},{28,24},{5,1},{9,5},{13... | collective-permute-start | bytes 1572872 | tf_op jit(solution)/shard_map/ppermute | solution.py:17
Sparse Core Ops, SparseCore 0:
  59.2 25.5 reduce-scatter.1
where the time goes:
time: 150 us; the launch traced here: 149 us
  waiting for transfers between devices  56.1 us (37%)
  matrix products  44.3 us (30%)
  between operations  25.6 us (17%)
  starting transfers between devices  11.7 us (8%)
  blocking collectives  7.28 us (5%)
  other arithmetic  2.65 us (2%)
  local copies, waits for them, and re-layouts  1.74 us (1%)
    reduce_scatter x1, waiting for transfers between devices, shards(): lax.psum_scatter(partial_sum, 'chan', scatter_dimension=1, tiled=True)  24.9 us
    dot_general x8, matrix products, padded_term(): lax.dot_general(halfway, right, (((1,), (1,)), ((), ())), preferred_eleme...  22.8 us
    dot_general x8, matrix products, shards(): lax.dot_general(update[sector], pulled, (((0,), (0,)), ((), ())), preferr...  21.5 us
    ppermute x2, waiting for transfers between devices, padded_2(): before = lax.ppermute(last, axis, up)  20 us
    ppermute x2, waiting for transfers between devices, padded_2(): after = lax.ppermute(initial, axis, down)  11.2 us
    all_gather x1, blocking collectives, shards(): update = lax.all_gather(update_rows, 'chan', axis=1, tiled=True)  7.28 us
    ppermute x2, starting transfers between devices, padded_2(): after = lax.ppermute(initial, axis, down)  6.26 us
    ppermute x2, starting transfers between devices, padded_2(): before = lax.ppermute(last, axis, up)  5.37 us
  transfers between devices with their start and end apart: 5, of which 5 were waited for; matrix products, arithmetic and copies ran while one was open for 1% of the time, Pallas kernels for 0%

commit v1 on v0

v1 whole, which is shorter than its diff:
```python
import functools

import jax
import jax.numpy as jnp
from jax import lax
from jax.experimental import pallas as pl
from jax.experimental.pallas import tpu as pltpu
from jax.sharding import PartitionSpec as P

BF16 = jnp.bfloat16
F32 = jnp.float32


def swap_core(x):
    count = lax.axis_size("chan")
    return lax.ppermute(x, "chan", [(i, i ^ 1) for i in range(count) if i ^ 1 < count])


def swap_near(x):
    count = lax.axis_size("sec")
    return lax.ppermute(x, "sec", [(i, i ^ 1) for i in range(count) if i ^ 1 < count])


def pass_far(x):
    count = lax.axis_size("sec")
    pairs = []
    for s in range(count):
        t = s + 2 if s % 2 == 0 else s - 2
        if 0 <= t < count and s ^ 1 < count:
            pairs.append((s, t))
    return lax.ppermute(x, "sec", pairs)


def join(dst, parity, mine, other, width):
    @pl.when(parity == 0)
    def _():
        dst[:, :width] = mine[...]
        dst[:, width:] = other[...]

    @pl.when(parity == 1)
    def _():
        dst[:, :width] = other[...]
        dst[:, width:] = mine[...]


def sum_kernel(scal, own, near_m, near_o, far_m, far_o, left, right, keep, give, src, acc):
    step = pl.program_id(0)
    last = pl.num_programs(0) - 1
    width = keep.shape[1]
    parity = scal[0]

    @pl.when(step == 0)
    def _():
        src[0] = own[...]
        join(src.at[1], parity, near_m, near_o, width)
        join(src.at[2], parity, far_m, far_o, width)
        acc[...] = jnp.zeros_like(acc)

    source = src[scal[1 + step]]
    halfway = jnp.dot(left[0, 0], source, preferred_element_type=F32).astype(BF16)
    acc[...] += lax.dot_general(
        halfway, right[0, 0], (((1,), (1,)), ((), ())), preferred_element_type=F32
    )

    @pl.when(step == last)
    def _():
        @pl.when(parity == 0)
        def _():
            keep[...] = acc[:, :width]
            give[...] = acc[:, width:].astype(BF16)

        @pl.when(parity == 1)
        def _():
            keep[...] = acc[:, width:]
            give[...] = acc[:, :width].astype(BF16)


def channel_sum(scal, own, near_m, near_o, far_m, far_o, left, right):
    chans, _, pad, _ = left.shape
    half = pad // 2
    whole = pl.BlockSpec((pad, pad), lambda c, s: (0, 0))
    part = pl.BlockSpec((pad, half), lambda c, s: (0, 0))
    block = pl.BlockSpec((1, 1, pad, pad), lambda c, s: (c, 0, 0, 0))
    return pl.pallas_call(
        sum_kernel,
        grid_spec=pltpu.PrefetchScalarGridSpec(
            num_scalar_prefetch=1,
            grid=(chans,),
            in_specs=[whole, part, part, part, part, block, block],
            out_specs=[part, part],
            scratch_shapes=[pltpu.VMEM((3, pad, pad), BF16), pltpu.VMEM((pad, pad), F32)],
        ),
        out_shape=[
            jax.ShapeDtypeStruct((pad, half), F32),
            jax.ShapeDtypeStruct((pad, half), BF16),
        ],
        cost_estimate=pl.CostEstimate(
            flops=chans * 4 * pad**3, transcendentals=0, bytes_accessed=chans * 4 * pad * pad
        ),
        name="channel_sum",
    )(scal, own, near_m, near_o, far_m, far_o, left, right)


def rotate_kernel(scal, own_m, own_o, near_m, near_o, far_m, far_o, left, rows, new_left, src, bra):
    step = pl.program_id(0)
    width = own_m.shape[1]
    parity = scal[0]
    pad = src.shape[1]

    @pl.when(step == 0)
    def _():
        join(src.at[0], parity, own_m, own_o, width)
        join(src.at[1], parity, near_m, near_o, width)
        join(src.at[2], parity, far_m, far_o, width)
        bra[...] = src[0].T
        count = rows.shape[0]
        rows[...] = src[0, pl.ds(pl.multiple_of(scal[1] * count, count), count), :]

    ket = src[scal[2 + step]]
    pulled = jnp.dot(left[0, 0], ket, preferred_element_type=F32).astype(BF16)
    rotated = jnp.dot(bra[...], pulled, preferred_element_type=F32)
    new_left[0, 0] = (rotated * pad ** (-0.5)).astype(BF16)


def rotate(scal, own_m, own_o, near_m, near_o, far_m, far_o, left, share):
    chans, _, pad, _ = left.shape
    half = pad // 2
    part = pl.BlockSpec((pad, half), lambda c, s: (0, 0))
    block = pl.BlockSpec((1, 1, pad, pad), lambda c, s: (c, 0, 0, 0))
    return pl.pallas_call(
        rotate_kernel,
        grid_spec=pltpu.PrefetchScalarGridSpec(
            num_scalar_prefetch=1,
            grid=(chans,),
            in_specs=[part] * 6 + [block],
            out_specs=[pl.BlockSpec((share, pad), lambda c, s: (0, 0)), block],
            scratch_shapes=[pltpu.VMEM((3, pad, pad), BF16), pltpu.VMEM((pad, pad), BF16)],
        ),
        out_shape=[
            jax.ShapeDtypeStruct((share, pad), BF16),
            jax.ShapeDtypeStruct(left.shape, BF16),
        ],
        cost_estimate=pl.CostEstimate(
            flops=chans * 4 * pad**3, transcendentals=0, bytes_accessed=chans * 4 * pad * pad
        ),
        name="rotate",
    )(scal, own_m, own_o, near_m, near_o, far_m, far_o, left)


def shards(state_blocks, left_blocks, right_blocks, widths, step_sizes, shifts):
    pad = state_blocks.shape[1]
    half = pad // 2
    chan_count = lax.axis_size("chan")
    rank = lax.axis_index("chan")
    sector = lax.axis_index("sec")
    parity = rank % 2
    first = parity * half
    width = widths[0]
    positions = jnp.arange(pad, dtype=jnp.int32)
    within = positions < width
    inside = within[:, None] & within[None, :]
    states = jnp.where(inside, state_blocks[0], jnp.zeros_like(state_blocks[0]))
    states_m = lax.dynamic_slice_in_dim(states, first, half, 1)
    inside_m = lax.dynamic_slice_in_dim(inside, first, half, 1)

    near_offset = jnp.where(sector % 2 == 0, -1, 1)
    which = jnp.where(shifts == 0, 0, jnp.where(shifts == near_offset, 1, 2))

    near_m = swap_near(states_m)
    far_m = pass_far(near_m)
    near_o = swap_core(near_m)
    far_o = swap_core(far_m)
    scal = jnp.concatenate([parity[None], which]).astype(jnp.int32)
    keep, give = channel_sum(scal, states, near_m, near_o, far_m, far_o, left_blocks, right_blocks)
    pair_sum = (keep + swap_core(give).astype(F32)).astype(BF16)
    total = pair_sum.astype(F32)
    for turn in range(2, chan_count, 2):
        moved = lax.ppermute(
            pair_sum, "chan", [(i, (i + turn) % chan_count) for i in range(chan_count)]
        )
        total = total + moved.astype(F32)
    product = jnp.where(inside_m, total, jnp.zeros_like(total))
    corrected = states_m.astype(F32) - step_sizes[0] * product
    update_m = jnp.where(inside_m, corrected, jnp.zeros_like(corrected)).astype(BF16)

    unear_m = swap_near(update_m)
    ufar_m = pass_far(unear_m)
    update_o = swap_core(update_m)
    unear_o = swap_core(unear_m)
    ufar_o = swap_core(ufar_m)
    scal = jnp.concatenate([parity[None], rank[None], which]).astype(jnp.int32)
    rows, new_left = rotate(
        scal, update_m, update_o, unear_m, unear_o, ufar_m, ufar_o, left_blocks, pad // chan_count
    )
    return rows[None], new_left


def solution(mesh):
    placed = (
        P("sec", None, None),
        P("chan", "sec", None, None),
        P("chan", "sec", None, None),
        P("sec"),
        P("sec"),
        P("chan"),
    )
    return jax.shard_map(
        shards,
        mesh=mesh,
        in_specs=placed,
        out_specs=(P("sec", "chan", None), P("chan", "sec", None, None)),
        check_vma=False,
    )
```

time: 150 us -> 77.5 us (0.52)
  matrix products: 44.3 us -> 0 us
  waiting for transfers between devices: 56.1 us -> 25.1 us
  between operations: 25.6 us -> 2.09 us
  Pallas kernels: 0 us -> 22.1 us
  starting transfers between devices: 11.7 us -> 19.5 us
  blocking collectives: 7.28 us -> 0 us
  other arithmetic: 2.65 us -> 5.65 us
    dot_general x16 -> x0, matrix products: 44.3 us -> none  [the longest x8 22.8 us: padded_term(): lax.dot_general(halfway, right, (((1,), (1,)), ((), ())), preferred_eleme...]
    reduce_scatter x1 -> x0, waiting for transfers between devices: 24.9 us -> none  [shards(): lax.psum_scatter(partial_sum, 'chan', scatter_dimension=1, tiled=True)]
    pallas_call x0 -> x2, Pallas kernels: none -> 22.1 us  [the longest x1 11.1 us: rotate(): pl.pallas_call(rotate_kernel, grid_spec=pltpu.PrefetchScalarGridSpec(num_...]
    ppermute x4 -> x11, starting transfers between devices: 11.6 us -> 19.5 us  [the longest x6 9.26 us: swap_core(): lax.ppermute(x, 'chan', [(i, i ^ 1) for i in range(count) if i ^ 1 < count])]
    all_gather x1 -> x0, blocking collectives: 7.28 us -> none  [shards(): update = lax.all_gather(update_rows, 'chan', axis=1, tiled=True)]
    ppermute x4 -> x11, waiting for transfers between devices: 31.2 us -> 25.1 us  [the longest x2 11.6 us: swap_near(): lax.ppermute(x, 'sec', [(i, i ^ 1) for i in range(count) if i ^ 1 < count])]
    unnamed x4 -> x22, local copies, waits for them, and re-layouts: 0.08 us -> 2.32 us
    slice x1 -> x0, local copies, waits for them, and re-layouts: 1.63 us -> none  [shards(): offset = shifts[channel]]
  transfers between devices with their start and end apart: 5 -> 11, of which waited for: 5 -> 7; matrix products, arithmetic and copies ran while one was open for 1% -> 3% of each run, Pallas kernels for 0% -> 0%
where the time goes in v1:
time: 77.5 us; the launch traced here: 76.8 us
  waiting for transfers between devices  25.1 us (32%)
  Pallas kernels  22.1 us (29%)
  starting transfers between devices  19.5 us (25%)
  other arithmetic  5.65 us (7%)
  local copies, waits for them, and re-layouts  2.35 us (3%)
  between operations  2.09 us (3%)
    ppermute x2, waiting for transfers between devices, swap_near(): lax.ppermute(x, 'sec', [(i, i ^ 1) for i in range(count) if i ^ 1 < count])  11.6 us
    pallas_call x1, Pallas kernels, rotate(): pl.pallas_call(rotate_kernel, grid_spec=pltpu.PrefetchScalarGridSpec(num_...  11.1 us
    pallas_call x1, Pallas kernels, channel_sum(): pl.pallas_call(sum_kernel, grid_spec=pltpu.PrefetchScalarGridSpec(num_sca...  11 us
    ppermute x6, starting transfers between devices, swap_core(): lax.ppermute(x, 'chan', [(i, i ^ 1) for i in range(count) if i ^ 1 < count])  9.26 us
    ppermute x2, starting transfers between devices, pass_far(): return lax.ppermute(x, 'sec', pairs)  6.39 us
    ppermute x1, waiting for transfers between devices, shards(): lax.ppermute(pair_sum, 'chan', [(i, (i + turn) % chan_count) for i in ran...  5.64 us
    ppermute x2, waiting for transfers between devices, pass_far(): return lax.ppermute(x, 'sec', pairs)  5.56 us
    ppermute x2, starting transfers between devices, swap_near(): lax.ppermute(x, 'sec', [(i, i ^ 1) for i in range(count) if i ^ 1 < count])  2.55 us
  transfers between devices with their start and end apart: 11, of which 7 were waited for; matrix products, arithmetic and copies ran while one was open for 3% of the time, Pallas kernels for 0%

profile of v1, /device:TPU:9, one launch (start us, length us, event | category | flops | bytes accessed | tf_op | source)
XLA Modules:
  0.0 76.8 jit_solution(11996784139493003726)
XLA Ops:
  1.3 1.3 %bitcast_select_fusion.own = bf16[512,512]{1,0:T(8,128)(2,1)S(1)} fusion(bf16[1,512,512]{2,1,0:T(8,128)(2,1)} %param.6, pred[512]{0:T(512)(128)(4,1)S(1)} %iota_compare_fusion), kind=kLoop, calls=%fused_computation | loop fusion | flops 524288 | bytes 1049088 | tf_op jit(solution)/shard_map/jit(_where)/select_n | solution.py:162
  2.6 1.3 %collective-permute-start = (bf16[512,256]{1,0:T(8,128)(2,1)S(1)}, bf16[512,256]{1,0:T(8,128)(2,1)S(1)}, u32[]{:S(2)}, u32[]{:S(2)}) collective-permute-start(bf16[512,256]{1,0:T(8,128)(2,1)S(1)} %constant_dynamic-slice_fusion), channel_id=1, source_target_pairs={{0,4},{4,0},{8,12},{12,8},{16,20},{20,16},{24,28},{28,24},{1,5},{5... | collective-permute-start | bytes 786440 | tf_op jit(solution)/shard_map/ppermute | solution.py:21
  3.9 6.0 %collective-permute-done.near_m = bf16[512,256]{1,0:T(8,128)(2,1)S(1)} collective-permute-done((bf16[512,256]{1,0:T(8,128)(2,1)S(1)}, bf16[512,256]{1,0:T(8,128)(2,1)S(1)}, u32[]{:S(2)}, u32[]{:S(2)}) %collective-permute-start) | collective-permute-done | bytes 262176 | tf_op jit(solution)/shard_map/ppermute | solution.py:21
  9.9 3.2 %collective-permute-start.2 = (bf16[512,256]{1,0:T(8,128)(2,1)S(1)}, bf16[512,256]{1,0:T(8,128)(2,1)S(1)}, u32[]{:S(2)}, u32[]{:S(2)}) collective-permute-start(bf16[512,256]{1,0:T(8,128)(2,1)S(1)} %collective-permute-done.near_m), channel_id=1, source_target_pairs={{0,8},{8,16},{12,4},{16,24},{20,12},{28,20},{1,9},{9,17},{13,5},{1... | collective-permute-start | bytes 786440 | tf_op jit(solution)/shard_map/ppermute | solution.py:31
  13.1 1.9 %collective-permute-start.1 = (bf16[512,256]{1,0:T(8,128)(2,1)S(1)}, bf16[512,256]{1,0:T(8,128)(2,1)S(1)}, u32[]{:S(2)}, u32[]{:S(2)}) collective-permute-start(bf16[512,256]{1,0:T(8,128)(2,1)S(1)} %collective-permute-done.near_m), channel_id=1, source_target_pairs={{0,1},{1,0},{2,3},{3,2},{4,5},{5,4},{6,7},{7,6},{8,9},{9,8},{10,11... | collective-permute-start | bytes 786440 | tf_op jit(solution)/shard_map/ppermute | solution.py:16
  15.0 3.1 %collective-permute-done.2.far_m = bf16[512,256]{1,0:T(8,128)(2,1)S(1)} collective-permute-done((bf16[512,256]{1,0:T(8,128)(2,1)S(1)}, bf16[512,256]{1,0:T(8,128)(2,1)S(1)}, u32[]{:S(2)}, u32[]{:S(2)}) %collective-permute-start.2) | collective-permute-done | bytes 262176 | tf_op jit(solution)/shard_map/ppermute | solution.py:31
  18.1 2.4 %collective-permute-start.3 = (bf16[512,256]{1,0:T(8,128)(2,1)S(1)}, bf16[512,256]{1,0:T(8,128)(2,1)S(1)}, u32[]{:S(2)}, u32[]{:S(2)}) collective-permute-start(bf16[512,256]{1,0:T(8,128)(2,1)S(1)} %collective-permute-done.2.far_m), channel_id=1, source_target_pairs={{0,1},{1,0},{2,3},{3,2},{4,5},{5,4},{6,7},{7,6},{8,9},{9,8},{10,11... | collective-permute-start | bytes 786440 | tf_op jit(solution)/shard_map/ppermute | solution.py:16
  20.5 0.7 compare_select_fusion.1
  21.1 0.7 pad_add_fusion.1.scal
  21.8 0.7 copy-done.8
  22.5 0.7 copy-done.10
  23.2 11.0 %channel_sum.1 = (f32[512,256]{1,0:T(8,128)}, bf16[512,256]{1,0:T(8,128)(2,1)}) custom-call(s32[9]{0:T(128)} %pad_add_fusion.1.scal, bf16[512,512]{1,0:T(8,128)(2,1)} %copy-done, bf16[512,256]{1,0:T(8,128)(2,1)} %copy-done.2, bf16[512,256]{1,0:T(8,128)(2,1)} %copy-done.8, bf16[512,256]{1,0:T(8,128)(2,1)} %copy-done.3, bf16[512,256]{1,0:T(8,128)(2,1)} %copy-done.10, ...), custom_call_target="tpu_custom_call" | custom-call | flops 4294967296 | bytes 8388608 | tf_op jit(solution)/shard_map/channel_sum/pallas_call | solution.py:84
  34.2 0.0 collective-permute-start.4
  34.2 1.7 %collective-permute-done.4 = bf16[512,256]{1,0:T(8,128)(2,1)S(1)} collective-permute-done((bf16[512,256]{1,0:T(8,128)(2,1)}, bf16[512,256]{1,0:T(8,128)(2,1)S(1)}, u32[]{:S(2)}, u32[]{:S(2)}) %collective-permute-start.4) | collective-permute-done | bytes 262176 | tf_op jit(solution)/shard_map/ppermute | solution.py:16
  35.9 1.1 %add_convert_fusion = bf16[512,256]{1,0:T(8,128)(2,1)S(1)} fusion(f32[512,256]{1,0:T(8,128)} %get-tuple-element.6, bf16[512,256]{1,0:T(8,128)(2,1)S(1)} %collective-permute-done.4), kind=kLoop, calls=%fused_computation.2 | loop fusion | flops 393216 | bytes 1048576 | tf_op jit(solution)/shard_map/convert_element_type | solution.py:175
  37.0 1.3 %collective-permute-start.5 = (bf16[512,256]{1,0:T(8,128)(2,1)S(1)}, bf16[512,256]{1,0:T(8,128)(2,1)S(1)}, u32[]{:S(2)}, u32[]{:S(2)}) collective-permute-start(bf16[512,256]{1,0:T(8,128)(2,1)S(1)} %add_convert_fusion), channel_id=1, source_target_pairs={{0,2},{1,3},{2,0},{3,1},{4,6},{5,7},{6,4},{7,5},{8,10},{9,11},{10,... | collective-permute-start | bytes 786440 | tf_op jit(solution)/shard_map/ppermute | solution.py:178
  39.0 0.2 broadcast_and_fusion
  39.2 5.6 %collective-permute-done.5 = bf16[512,256]{1,0:T(8,128)(2,1)S(1)} collective-permute-done((bf16[512,256]{1,0:T(8,128)(2,1)S(1)}, bf16[512,256]{1,0:T(8,128)(2,1)S(1)}, u32[]{:S(2)}, u32[]{:S(2)}) %collective-permute-start.5) | collective-permute-done | bytes 262176 | tf_op jit(solution)/shard_map/ppermute | solution.py:178
  44.8 1.2 %select_convert_fusion.own_m = bf16[512,256]{1,0:T(8,128)(2,1)S(1)} fusion(bf16[512,256]{1,0:T(8,128)(2,1)S(1)} %collective-permute-done.5, bf16[512,256]{1,0:T(8,128)(2,1)S(1)} %add_convert_fusion, pred[512,512]{1,0:T(8,128)(4,1)S(1)} %broadcast_and_fusion, s32[]{:T(128)S(6)} %select_n.43, f32[]{:T(128)} %bitcast.8, bf16[512,512]{1,0:T(8,128)(2,1)} %copy-done), kind=kLoop, calls=%fused_computation.1 | loop fusion | flops 1179648 | bytes 1179656 | tf_op jit(solution)/shard_map/convert_element_type | solution.py:184
  46.0 1.3 %collective-permute-start.7 = (bf16[512,256]{1,0:T(8,128)(2,1)S(1)}, bf16[512,256]{1,0:T(8,128)(2,1)S(1)}, u32[]{:S(2)}, u32[]{:S(2)}) collective-permute-start(bf16[512,256]{1,0:T(8,128)(2,1)S(1)} %select_convert_fusion.own_m), channel_id=1, source_target_pairs={{0,4},{4,0},{8,12},{12,8},{16,20},{20,16},{24,28},{28,24},{1,5},{5... | collective-permute-start | bytes 786440 | tf_op jit(solution)/shard_map/ppermute | solution.py:21
  47.3 5.7 %collective-permute-done.7.near_m = bf16[512,256]{1,0:T(8,128)(2,1)S(1)} collective-permute-done((bf16[512,256]{1,0:T(8,128)(2,1)S(1)}, bf16[512,256]{1,0:T(8,128)(2,1)S(1)}, u32[]{:S(2)}, u32[]{:S(2)}) %collective-permute-start.7) | collective-permute-done | bytes 262176 | tf_op jit(solution)/shard_map/ppermute | solution.py:21
  52.9 3.2 %collective-permute-start.9 = (bf16[512,256]{1,0:T(8,128)(2,1)S(1)}, bf16[512,256]{1,0:T(8,128)(2,1)S(1)}, u32[]{:S(2)}, u32[]{:S(2)}) collective-permute-start(bf16[512,256]{1,0:T(8,128)(2,1)S(1)} %collective-permute-done.7.near_m), channel_id=1, source_target_pairs={{0,8},{8,16},{12,4},{16,24},{20,12},{28,20},{1,9},{9,17},{13,5},{1... | collective-permute-start | bytes 786440 | tf_op jit(solution)/shard_map/ppermute | solution.py:31
  56.1 2.2 %collective-permute-start.6 = (bf16[512,256]{1,0:T(8,128)(2,1)S(1)}, bf16[512,256]{1,0:T(8,128)(2,1)S(1)}, u32[]{:S(2)}, u32[]{:S(2)}) collective-permute-start(bf16[512,256]{1,0:T(8,128)(2,1)S(1)} %select_convert_fusion.own_m), channel_id=1, source_target_pairs={{0,1},{1,0},{2,3},{3,2},{4,5},{5,4},{6,7},{7,6},{8,9},{9,8},{10,11... | collective-permute-start | bytes 786440 | tf_op jit(solution)/shard_map/ppermute | solution.py:16
  58.3 0.1 collective-permute-start.8
  58.4 2.4 %collective-permute-done.9.far_m = bf16[512,256]{1,0:T(8,128)(2,1)S(1)} collective-permute-done((bf16[512,256]{1,0:T(8,128)(2,1)S(1)}, bf16[512,256]{1,0:T(8,128)(2,1)S(1)}, u32[]{:S(2)}, u32[]{:S(2)}) %collective-permute-start.9) | collective-permute-done | bytes 262176 | tf_op jit(solution)/shard_map/ppermute | solution.py:31
  60.8 2.7 %collective-permute-start.10 = (bf16[512,256]{1,0:T(8,128)(2,1)S(1)}, bf16[512,256]{1,0:T(8,128)(2,1)S(1)}, u32[]{:S(2)}, u32[]{:S(2)}) collective-permute-start(bf16[512,256]{1,0:T(8,128)(2,1)S(1)} %collective-permute-done.9.far_m), channel_id=1, source_target_pairs={{0,1},{1,0},{2,3},{3,2},{4,5},{5,4},{6,7},{7,6},{8,9},{9,8},{10,11... | collective-permute-start | bytes 786440 | tf_op jit(solution)/shard_map/ppermute | solution.py:16
  63.5 0.6 pad_add_fusion.scal
  64.2 0.5 collective-permute-done.10.far_o
  64.7 0.1 copy-done.6
  64.9 0.1 copy-done.7
  65.0 0.7 copy-done.9
  65.7 11.1 %rotate.1 = (bf16[128,512]{1,0:T(8,128)(2,1)}, bf16[8,1,512,512]{3,2,1,0:T(8,128)(2,1)}) custom-call(s32[10]{0:T(128)} %pad_add_fusion.scal, bf16[512,256]{1,0:T(8,128)(2,1)} %copy-done.1, bf16[512,256]{1,0:T(8,128)(2,1)} %copy-done.6, bf16[512,256]{1,0:T(8,128)(2,1)} %copy-done.4, bf16[512,256]{1,0:T(8,128)(2,1)} %copy-done.7, bf16[512,256]{1,0:T(8,128)(2,1)} %copy-done.5, ...), custom_call_target="tpu_custom_call" | custom-call | flops 4294967296 | bytes 8388608 | tf_op jit(solution)/shard_map/rotate/pallas_call | solution.py:130
  (23 shorter events, 0.1 us)
Async XLA Ops:
  2.6 19.2 %copy-start = (bf16[512,512]{1,0:T(8,128)(2,1)}, bf16[512,512]{1,0:T(8,128)(2,1)S(1)}, u32[]{:S(2)}) copy-start(bf16[512,512]{1,0:T(8,128)(2,1)S(1)} %bitcast_select_fusion.own) | copy-start | bytes 1572868
  2.6 7.3 %collective-permute-start = (bf16[512,256]{1,0:T(8,128)(2,1)S(1)}, bf16[512,256]{1,0:T(8,128)(2,1)S(1)}, u32[]{:S(2)}, u32[]{:S(2)}) collective-permute-start(bf16[512,256]{1,0:T(8,128)(2,1)S(1)} %constant_dynamic-slice_fusion), channel_id=1, source_target_pairs={{0,4},{4,0},{8,12},{12,8},{16,20},{20,16},{24,28},{28,24},{1,5},{5... | collective-permute-start | bytes 786440 | tf_op jit(solution)/shard_map/ppermute | solution.py:21
  9.9 11.9 %copy-start.2 = (bf16[512,256]{1,0:T(8,128)(2,1)}, bf16[512,256]{1,0:T(8,128)(2,1)S(1)}, u32[]{:S(2)}) copy-start(bf16[512,256]{1,0:T(8,128)(2,1)S(1)} %collective-permute-done.near_m) | copy-start | bytes 786436
  9.9 8.2 %collective-permute-start.2 = (bf16[512,256]{1,0:T(8,128)(2,1)S(1)}, bf16[512,256]{1,0:T(8,128)(2,1)S(1)}, u32[]{:S(2)}, u32[]{:S(2)}) collective-permute-start(bf16[512,256]{1,0:T(8,128)(2,1)S(1)} %collective-permute-done.near_m), channel_id=1, source_target_pairs={{0,8},{8,16},{12,4},{16,24},{20,12},{28,20},{1,9},{9,17},{13,5},{1... | collective-permute-start | bytes 786440 | tf_op jit(solution)/shard_map/ppermute | solution.py:31
  13.1 8.7 %collective-permute-start.1 = (bf16[512,256]{1,0:T(8,128)(2,1)S(1)}, bf16[512,256]{1,0:T(8,128)(2,1)S(1)}, u32[]{:S(2)}, u32[]{:S(2)}) collective-permute-start(bf16[512,256]{1,0:T(8,128)(2,1)S(1)} %collective-permute-done.near_m), channel_id=1, source_target_pairs={{0,1},{1,0},{2,3},{3,2},{4,5},{5,4},{6,7},{7,6},{8,9},{9,8},{10,11... | collective-permute-start | bytes 786440 | tf_op jit(solution)/shard_map/ppermute | solution.py:16
  18.1 3.7 %copy-start.3 = (bf16[512,256]{1,0:T(8,128)(2,1)}, bf16[512,256]{1,0:T(8,128)(2,1)S(1)}, u32[]{:S(2)}) copy-start(bf16[512,256]{1,0:T(8,128)(2,1)S(1)} %collective-permute-done.2.far_m) | copy-start | bytes 786436
  18.1 3.7 %collective-permute-start.3 = (bf16[512,256]{1,0:T(8,128)(2,1)S(1)}, bf16[512,256]{1,0:T(8,128)(2,1)S(1)}, u32[]{:S(2)}, u32[]{:S(2)}) collective-permute-start(bf16[512,256]{1,0:T(8,128)(2,1)S(1)} %collective-permute-done.2.far_m), channel_id=1, source_target_pairs={{0,1},{1,0},{2,3},{3,2},{4,5},{5,4},{6,7},{7,6},{8,9},{9,8},{10,11... | collective-permute-start | bytes 786440 | tf_op jit(solution)/shard_map/ppermute | solution.py:16
  21.8 0.7 copy-start.8
  22.5 0.7 copy-start.10
  34.2 1.7 %collective-permute-start.4 = (bf16[512,256]{1,0:T(8,128)(2,1)}, bf16[512,256]{1,0:T(8,128)(2,1)S(1)}, u32[]{:S(2)}, u32[]{:S(2)}) collective-permute-start(bf16[512,256]{1,0:T(8,128)(2,1)} %get-tuple-element.7), channel_id=1, source_target_pairs={{0,1},{1,0},{2,3},{3,2},{4,5},{5,4},{6,7},{7,6},{8,9},{9,8},{10,11... | collective-permute-start | bytes 786440 | tf_op jit(solution)/shard_map/ppermute | solution.py:16
  37.0 7.8 %collective-permute-start.5 = (bf16[512,256]{1,0:T(8,128)(2,1)S(1)}, bf16[512,256]{1,0:T(8,128)(2,1)S(1)}, u32[]{:S(2)}, u32[]{:S(2)}) collective-permute-start(bf16[512,256]{1,0:T(8,128)(2,1)S(1)} %add_convert_fusion), channel_id=1, source_target_pairs={{0,2},{1,3},{2,0},{3,1},{4,6},{5,7},{6,4},{7,5},{8,10},{9,11},{10,... | collective-permute-start | bytes 786440 | tf_op jit(solution)/shard_map/ppermute | solution.py:178
  46.0 18.7 %copy-start.1 = (bf16[512,256]{1,0:T(8,128)(2,1)}, bf16[512,256]{1,0:T(8,128)(2,1)S(1)}, u32[]{:S(2)}) copy-start(bf16[512,256]{1,0:T(8,128)(2,1)S(1)} %select_convert_fusion.own_m) | copy-start | bytes 786436
  46.0 6.9 %collective-permute-start.7 = (bf16[512,256]{1,0:T(8,128)(2,1)S(1)}, bf16[512,256]{1,0:T(8,128)(2,1)S(1)}, u32[]{:S(2)}, u32[]{:S(2)}) collective-permute-start(bf16[512,256]{1,0:T(8,128)(2,1)S(1)} %select_convert_fusion.own_m), channel_id=1, source_target_pairs={{0,4},{4,0},{8,12},{12,8},{16,20},{20,16},{24,28},{28,24},{1,5},{5... | collective-permute-start | bytes 786440 | tf_op jit(solution)/shard_map/ppermute | solution.py:21
  52.9 11.8 %copy-start.4 = (bf16[512,256]{1,0:T(8,128)(2,1)}, bf16[512,256]{1,0:T(8,128)(2,1)S(1)}, u32[]{:S(2)}) copy-start(bf16[512,256]{1,0:T(8,128)(2,1)S(1)} %collective-permute-done.7.near_m) | copy-start | bytes 786436
  52.9 7.9 %collective-permute-start.9 = (bf16[512,256]{1,0:T(8,128)(2,1)S(1)}, bf16[512,256]{1,0:T(8,128)(2,1)S(1)}, u32[]{:S(2)}, u32[]{:S(2)}) collective-permute-start(bf16[512,256]{1,0:T(8,128)(2,1)S(1)} %collective-permute-done.7.near_m), channel_id=1, source_target_pairs={{0,8},{8,16},{12,4},{16,24},{20,12},{28,20},{1,9},{9,17},{13,5},{1... | collective-permute-start | bytes 786440 | tf_op jit(solution)/shard_map/ppermute | solution.py:31
  56.1 8.0 %collective-permute-start.6 = (bf16[512,256]{1,0:T(8,128)(2,1)S(1)}, bf16[512,256]{1,0:T(8,128)(2,1)S(1)}, u32[]{:S(2)}, u32[]{:S(2)}) collective-permute-start(bf16[512,256]{1,0:T(8,128)(2,1)S(1)} %select_convert_fusion.own_m), channel_id=1, source_target_pairs={{0,1},{1,0},{2,3},{3,2},{4,5},{5,4},{6,7},{7,6},{8,9},{9,8},{10,11... | collective-permute-start | bytes 786440 | tf_op jit(solution)/shard_map/ppermute | solution.py:16
  58.3 5.8 %collective-permute-start.8 = (bf16[512,256]{1,0:T(8,128)(2,1)S(1)}, bf16[512,256]{1,0:T(8,128)(2,1)S(1)}, u32[]{:S(2)}, u32[]{:S(2)}) collective-permute-start(bf16[512,256]{1,0:T(8,128)(2,1)S(1)} %collective-permute-done.7.near_m), channel_id=1, source_target_pairs={{0,1},{1,0},{2,3},{3,2},{4,5},{5,4},{6,7},{7,6},{8,9},{9,8},{10,11... | collective-permute-start | bytes 786440 | tf_op jit(solution)/shard_map/ppermute | solution.py:16
  60.8 3.9 %copy-start.5 = (bf16[512,256]{1,0:T(8,128)(2,1)}, bf16[512,256]{1,0:T(8,128)(2,1)S(1)}, u32[]{:S(2)}) copy-start(bf16[512,256]{1,0:T(8,128)(2,1)S(1)} %collective-permute-done.9.far_m) | copy-start | bytes 786436
  60.8 3.9 %collective-permute-start.10 = (bf16[512,256]{1,0:T(8,128)(2,1)S(1)}, bf16[512,256]{1,0:T(8,128)(2,1)S(1)}, u32[]{:S(2)}, u32[]{:S(2)}) collective-permute-start(bf16[512,256]{1,0:T(8,128)(2,1)S(1)} %collective-permute-done.9.far_m), channel_id=1, source_target_pairs={{0,1},{1,0},{2,3},{3,2},{4,5},{5,4},{6,7},{7,6},{8,9},{9,8},{10,11... | collective-permute-start | bytes 786440 | tf_op jit(solution)/shard_map/ppermute | solution.py:16
  64.2 0.7 copy-start.6
  64.2 0.8 %copy-start.7 = (bf16[512,256]{1,0:T(8,128)(2,1)}, bf16[512,256]{1,0:T(8,128)(2,1)S(1)}, u32[]{:S(2)}) copy-start(bf16[512,256]{1,0:T(8,128)(2,1)S(1)} %collective-permute-done.8.near_o) | copy-start | bytes 786436
  65.0 0.7 copy-start.9

commit v2 on v0

v2 whole, which is shorter than its diff:
```python
import functools

import jax
import jax.numpy as jnp
from jax import lax
from jax.experimental import pallas as pl
from jax.experimental.pallas import tpu as pltpu
from jax.sharding import PartitionSpec as P


BF16 = jnp.bfloat16
F32 = jnp.float32
OWN, NEAR, FAR = 0, 1, 2
ROOM = 28 << 20
VMEM = pl.BlockSpec(memory_space=pltpu.VMEM)
SMEM = pl.BlockSpec(memory_space=pltpu.SMEM)
ANY = pl.BlockSpec(memory_space=pl.ANY)


def held(x):
    return pltpu.with_memory_space_constraint(x, pltpu.VMEM)


def swap_core(x):
    count = lax.axis_size("chan")
    return lax.ppermute(x, "chan", [(i, i ^ 1) for i in range(count) if i ^ 1 < count])


def swap_near(x):
    count = lax.axis_size("sec")
    return lax.ppermute(x, "sec", [(i, i ^ 1) for i in range(count) if i ^ 1 < count])


def pass_far(x):
    count = lax.axis_size("sec")
    pairs = [(s, s + 2 if s % 2 == 0 else s - 2) for s in range(count)]
    pairs = [(s, t) for s, t in pairs if 0 <= t < count]
    sources = sorted(set(range(count)) - {s for s, _ in pairs})
    targets = sorted(set(range(count)) - {t for _, t in pairs})
    return lax.ppermute(x, "sec", pairs + list(zip(sources, targets)))


def far_exists():
    sector = lax.axis_index("sec")
    far = sector + 1 - 2 * lax.rem(sector + 1, 2)
    return (far >= 0) & (far < lax.axis_size("sec"))


def place(offset):
    near = 2 * lax.rem(lax.axis_index("sec"), 2) - 1
    return jnp.where(offset == 0, OWN, jnp.where(offset == near, NEAR, FAR))


def list_channels(shifts, order, wanted, start=0):
    count = jnp.int32(start)
    for channel in range(shifts.shape[0]):
        order[count] = channel
        count += jnp.where(place(shifts[channel]) == wanted, 1, 0)
    return count


def join(dst, mine, other, valid=None):
    parity = lax.rem(lax.axis_index("chan"), 2)
    half = mine.shape[0]
    dst[pl.ds(pl.multiple_of(parity * half, half), half), :] = mine[...]
    dst[pl.ds(pl.multiple_of((1 - parity) * half, half), half), :] = other[...]
    if valid is not None:

        @pl.when(jnp.logical_not(valid))
        def _():
            dst[...] = jnp.zeros_like(dst)


def add_terms(count, order, src, left, right, acc, ready):
    def body(i, carry):
        channel = order[i]
        ready(channel)
        halfway = jnp.dot(left[channel], src[...], preferred_element_type=F32).astype(BF16)
        acc[...] += lax.dot_general(
            halfway, right[channel], (((1,), (1,)), ((), ())), preferred_element_type=F32
        )
        return carry

    lax.fori_loop(0, count, body, 0)


def own_sum_kernel(
    shifts_in, widths_in, state_in, left_in, right_in, acc, left, right,
    src, shifts, widths, order, small_sem, left_sem, right_sem
):
    small = [
        pltpu.make_async_copy(shifts_in, shifts, small_sem.at[0]),
        pltpu.make_async_copy(widths_in, widths, small_sem.at[1]),
        pltpu.make_async_copy(state_in.at[0], src, small_sem.at[2]),
    ]
    for copy in small:
        copy.start()

    def loads(channel):
        return (
            pltpu.make_async_copy(left_in.at[channel, 0], left.at[channel], left_sem.at[channel]),
            pltpu.make_async_copy(right_in.at[channel, 0], right.at[channel], right_sem.at[channel]),
        )

    small[0].wait()
    owned = list_channels(shifts, order, OWN)
    near = list_channels(shifts, order, NEAR, owned)
    list_channels(shifts, order, FAR, near)

    def fetch(i, carry):
        for copy in loads(order[i]):
            copy.start()
        return carry

    lax.fori_loop(0, left.shape[0], fetch, 0)
    acc[...] = jnp.zeros_like(acc)
    small[1].wait()
    small[2].wait()
    rows = lax.broadcasted_iota(jnp.int32, src.shape, 0)
    cols = lax.broadcasted_iota(jnp.int32, src.shape, 1)
    inside = (rows < widths[0]) & (cols < widths[0])
    src[...] = jnp.where(inside, src[...], jnp.zeros_like(src))

    def ready(channel):
        for copy in loads(channel):
            copy.wait()

    add_terms(owned, order, src, left, right, acc, ready)

    def rest(i, carry):
        ready(order[i])
        return carry

    lax.fori_loop(owned, left.shape[0], rest, 0)


def next_sum_kernel(wanted, last, shifts, mine, other, acc_in, left, right, *rest):
    if last:
        keep, give, acc, src, order = rest
    else:
        acc, src, order = rest
    count = list_channels(shifts, order, wanted)
    join(src, mine, other, far_exists() if last else None)
    acc[...] = acc_in[...]
    add_terms(count, order, src, left, right, acc, lambda channel: None)
    if last:
        half = keep.shape[0]
        parity = lax.rem(lax.axis_index("chan"), 2)
        keep[...] = acc[pl.ds(pl.multiple_of(parity * half, half), half), :]
        give[...] = acc[pl.ds(pl.multiple_of((1 - parity) * half, half), half), :].astype(BF16)


def cost(matmuls, pad):
    return pl.CostEstimate(
        flops=int(matmuls * 2 * pad**3), transcendentals=0, bytes_accessed=int(matmuls * 2 * pad**2)
    )


def own_sum(shifts, widths, state, left, right):
    chans, _, pad, _ = left.shape
    blocks = jax.ShapeDtypeStruct((chans, pad, pad), BF16)
    return pl.pallas_call(
        own_sum_kernel,
        in_specs=[ANY] * 5,
        out_specs=[VMEM] * 3,
        out_shape=[jax.ShapeDtypeStruct((pad, pad), F32), blocks, blocks],
        scratch_shapes=[
            pltpu.VMEM((pad, pad), BF16),
            pltpu.SMEM(shifts.shape, jnp.int32),
            pltpu.SMEM(widths.shape, jnp.int32),
            pltpu.SMEM((chans + 1,), jnp.int32),
            pltpu.SemaphoreType.DMA((3,)),
            pltpu.SemaphoreType.DMA((chans,)),
            pltpu.SemaphoreType.DMA((chans,)),
        ],
        compiler_params=pltpu.CompilerParams(vmem_limit_bytes=ROOM),
        cost_estimate=cost(2 * chans / 3, pad),
        name="own_sum",
    )(shifts, widths, *[pltpu.with_memory_space_constraint(x, pltpu.HBM) for x in (state, left, right)])


def next_sum(wanted, last, shifts, mine, other, acc, left, right):
    chans, pad, _ = left.shape
    half = pad // 2
    whole = jax.ShapeDtypeStruct((pad, pad), F32)
    scratch = [pltpu.VMEM((pad, pad), BF16), pltpu.SMEM((chans + 1,), jnp.int32)]
    if last:
        scratch = [pltpu.VMEM((pad, pad), F32)] + scratch
    return pl.pallas_call(
        functools.partial(next_sum_kernel, wanted, last),
        in_specs=[SMEM] + [VMEM] * 5,
        out_specs=[VMEM, VMEM] if last else VMEM,
        out_shape=[
            jax.ShapeDtypeStruct((half, pad), F32),
            jax.ShapeDtypeStruct((half, pad), BF16),
        ]
        if last
        else whole,
        scratch_shapes=scratch,
        compiler_params=pltpu.CompilerParams(vmem_limit_bytes=ROOM),
        cost_estimate=cost(2 * chans / 3, pad),
        name="far_sum" if last else "near_sum",
    )(shifts, *[held(x) for x in (mine, other, acc, left, right)])


def finish(first, count, order, turned, src, new_left, obuf, osem, ready=None):
    scale = src.shape[0] ** (-0.5)

    def store(i):
        return pltpu.make_async_copy(obuf.at[i], new_left.at[order[i], 0], osem.at[i])

    def body(i, carry):
        bra_left = ready[i] if turned is None else turned(order[i])
        rotated = jnp.dot(bra_left, src[...], preferred_element_type=F32)
        obuf[i] = (rotated * scale).astype(BF16)
        store(i).start()
        return carry

    lax.fori_loop(first, count, body, 0)

    def drain(i, carry):
        store(i).wait()
        return carry

    return lambda: lax.fori_loop(first, count, drain, 0)


def turn(bra, left, channel):
    return jnp.dot(bra[...], left[channel], preferred_element_type=F32).astype(BF16)


def turn_ahead(shifts, order, wanted, bra, left, half_turned):
    count = list_channels(shifts, order, wanted)

    def body(i, carry):
        half_turned[i] = turn(bra, left, order[i])
        return carry

    lax.fori_loop(0, count, body, 0)


def own_turn_kernel(
    shifts, mine, other, left, rows, new_left, half_turned, bra, src, order, ahead, obuf, osem
):
    owned = list_channels(shifts, order, OWN)
    join(src, mine, other)
    bra[...] = src[...].T
    share = rows.shape[0]
    rows[...] = src[pl.ds(pl.multiple_of(lax.axis_index("chan") * share, share), share), :]
    drain = finish(
        0, owned, order, lambda channel: turn(bra, left, channel), src, new_left, obuf, osem
    )
    turn_ahead(shifts, ahead, NEAR, bra, left, half_turned)
    drain()


def turn_scratch(chans, pad):
    return [
        pltpu.VMEM((pad, pad), BF16),
        pltpu.SMEM((chans + 1,), jnp.int32),
        pltpu.SMEM((chans + 1,), jnp.int32),
        pltpu.VMEM((chans, pad, pad), BF16),
        pltpu.SemaphoreType.DMA((chans,)),
    ]


def own_turn(shifts, mine, other, left, share):
    chans, pad, _ = left.shape
    return pl.pallas_call(
        own_turn_kernel,
        in_specs=[SMEM, VMEM, VMEM, VMEM],
        out_specs=[VMEM, ANY, VMEM, VMEM],
        out_shape=[
            jax.ShapeDtypeStruct((share, pad), BF16),
            jax.ShapeDtypeStruct((chans, 1, pad, pad), BF16),
            jax.ShapeDtypeStruct((chans, pad, pad), BF16),
            jax.ShapeDtypeStruct((pad, pad), BF16),
        ],
        scratch_shapes=turn_scratch(chans, pad),
        compiler_params=pltpu.CompilerParams(vmem_limit_bytes=ROOM),
        cost_estimate=cost(chans, pad),
        name="own_turn",
    )(shifts, held(mine), held(other), held(left))


def near_turn_kernel(
    shifts, mine, other, half_turned, bra, left, old, new_left, far_turned, src, order, ahead, obuf, osem
):
    count = list_channels(shifts, order, NEAR)
    join(src, mine, other)
    drain = finish(0, count, order, None, src, new_left, obuf, osem, half_turned)
    turn_ahead(shifts, ahead, FAR, bra, left, far_turned)
    drain()


def near_turn(shifts, mine, other, half_turned, bra, left, new_left):
    chans, pad, _ = left.shape
    return pl.pallas_call(
        near_turn_kernel,
        in_specs=[SMEM] + [VMEM] * 5 + [ANY],
        out_specs=[ANY, VMEM],
        out_shape=[
            jax.ShapeDtypeStruct(new_left.shape, BF16),
            jax.ShapeDtypeStruct((chans, pad, pad), BF16),
        ],
        scratch_shapes=turn_scratch(chans, pad),
        input_output_aliases={6: 0},
        compiler_params=pltpu.CompilerParams(vmem_limit_bytes=ROOM),
        cost_estimate=cost(2 * chans / 3, pad),
        name="near_turn",
    )(shifts, *[held(x) for x in (mine, other, half_turned, bra, left)], new_left)


def far_turn_kernel(shifts, mine, other, far_turned, old, new_left, src, order, ahead, obuf, osem):
    count = list_channels(shifts, order, FAR)
    join(src, mine, other, far_exists())
    finish(0, count, order, None, src, new_left, obuf, osem, far_turned)()


def far_turn(shifts, mine, other, far_turned, new_left):
    chans, pad, _ = far_turned.shape
    return pl.pallas_call(
        far_turn_kernel,
        in_specs=[SMEM] + [VMEM] * 3 + [ANY],
        out_specs=ANY,
        out_shape=jax.ShapeDtypeStruct(new_left.shape, BF16),
        scratch_shapes=turn_scratch(chans, pad),
        input_output_aliases={4: 0},
        compiler_params=pltpu.CompilerParams(vmem_limit_bytes=ROOM),
        cost_estimate=cost(chans / 3, pad),
        name="far_turn",
    )(shifts, held(mine), held(other), held(far_turned), new_left)


def exchange(mine):
    near_a = swap_near(mine[: mine.shape[0] // 2])
    near_b = swap_near(mine[mine.shape[0] // 2 :])
    far_a = pass_far(near_a)
    far_b = pass_far(near_b)
    near = held(jnp.concatenate([near_a, near_b]))
    far = held(jnp.concatenate([far_a, far_b]))
    near_other = swap_core(near)
    far_other = swap_core(far)
    return near, near_other, far, far_other


def body(state_blocks, left_blocks, right_blocks, widths, step_sizes, shifts):
    pad = state_blocks.shape[1]
    half = pad // 2
    chan_count = lax.axis_size("chan")
    first = lax.axis_index("chan") % 2 * half
    width = widths[0]
    positions = jnp.arange(pad, dtype=jnp.int32)
    inside = ((first + positions[:half]) < width)[:, None] & (positions < width)[None, :]
    state_m = lax.dynamic_slice_in_dim(state_blocks[0], first, half, 0)
    state_m = jnp.where(inside, state_m, jnp.zeros_like(state_m))

    near_m, near_o, far_m, far_o = exchange(state_m)
    acc, left, right = own_sum(shifts, widths, state_blocks, left_blocks, right_blocks)
    acc = next_sum(NEAR, False, shifts, near_m, near_o, acc, left, right)
    keep, give = next_sum(FAR, True, shifts, far_m, far_o, acc, left, right)

    pair_sum = (keep + swap_core(give).astype(F32)).astype(BF16)
    total = pair_sum.astype(F32)
    for turn in range(2, chan_count, 2):
        moved = lax.ppermute(
            pair_sum, "chan", [(i, (i + turn) % chan_count) for i in range(chan_count)]
        )
        total = total + moved.astype(F32)
    product = jnp.where(inside, total, jnp.zeros_like(total))
    corrected = state_m.astype(F32) - step_sizes[0] * product
    update_m = jnp.where(inside, corrected, jnp.zeros_like(corrected)).astype(BF16)

    near_m, near_o, far_m, far_o = exchange(update_m)
    update_o = swap_core(update_m)
    rows, new_left, half_turned, bra = own_turn(shifts, update_m, update_o, left, pad // chan_count)
    new_left, far_turned = near_turn(
        shifts, near_m, near_o, half_turned, bra, left, new_left
    )
    new_left = far_turn(shifts, far_m, far_o, far_turned, new_left)
    return rows[None], new_left


def solution(mesh):
    placed = (
        P("sec", None, None),
        P("chan", "sec", None, None),
        P("chan", "sec", None, None),
        P("sec"),
        P("sec"),
        P("chan"),
    )
    return jax.shard_map(
        body,
        mesh=mesh,
        in_specs=placed,
        out_specs=(P("sec", "chan", None), P("chan", "sec", None, None)),
        check_vma=False,
    )
```

time: 150 us -> 64 us (0.43)
  the two profiles are of different devices: /device:TPU:9 before, /device:TPU:0 now
where the time goes in v2:
time: 64 us; the launch traced here: 63.9 us
  waiting for transfers between devices  26.7 us (42%)
  Pallas kernels  19.7 us (31%)
  starting transfers between devices  13.1 us (20%)
  between operations  2.18 us (3%)
  other arithmetic  1.42 us (2%)
  local copies, waits for them, and re-layouts  0.78 us (1%)
    ppermute x4, waiting for transfers between devices, swap_near(): lax.ppermute(x, 'sec', [(i, i ^ 1) for i in range(count) if i ^ 1 < count])  10.9 us
    ppermute x4, waiting for transfers between devices, pass_far(): return lax.ppermute(x, 'sec', pairs + list(zip(sources, targets)))  8.67 us
    ppermute x1, waiting for transfers between devices, body(): lax.ppermute(pair_sum, 'chan', [(i, (i + turn) % chan_count) for i in ran...  5.96 us
    ppermute x4, starting transfers between devices, swap_near(): lax.ppermute(x, 'sec', [(i, i ^ 1) for i in range(count) if i ^ 1 < count])  5.2 us
    pallas_call x1, Pallas kernels, own_turn(): pl.pallas_call(own_turn_kernel, in_specs=[SMEM, VMEM, VMEM, VMEM], out_sp...  5.15 us
    pallas_call x1, Pallas kernels, own_sum(): pl.pallas_call(own_sum_kernel, in_specs=[ANY] * 5, out_specs=[VMEM] * 3,...  4.91 us
    ppermute x4, starting transfers between devices, pass_far(): return lax.ppermute(x, 'sec', pairs + list(zip(sources, targets)))  4.39 us
    pallas_call x2, Pallas kernels, next_sum(): pl.pallas_call(functools.partial(next_sum_kernel, wanted, last), in_specs...  4.3 us
  transfers between devices with their start and end apart: 15, of which 10 were waited for; matrix products, arithmetic and copies ran while one was open for 0% of the time, Pallas kernels for 22%

profile of v2, /device:TPU:0, one launch (start us, length us, event | category | flops | bytes accessed | tf_op | source)
XLA Modules:
  0.0 63.9 jit_solution(3268104183731044907)
XLA Ops:
  1.3 1.1 %and_select_fusion.2 = bf16[256,512]{1,0:T(8,128)(2,1)S(1)} fusion(bf16[1,512,512]{2,1,0:T(8,128)(2,1)} %state_in.1, s32[]{:T(128)S(6)} %select_n.22, pred[512]{0:T(512)(128)(4,1)S(1)} %iota_compare_fusion, pred[256]{0:T(512)(128)(4,1)S(1)} %add_compare_fusion), kind=kLoop, calls=%fused_computation.2 | loop fusion | flops 262144 | bytes 525060 | tf_op jit(solution)/shard_map/jit(_where)/select_n | solution.py:356
  2.5 3.0 %collective-permute-start = (bf16[128,512]{1,0:T(8,128)(2,1)S(1)}, bf16[128,512]{1,0:T(8,128)(2,1)S(1)}, u32[]{:S(2)}, u32[]{:S(2)}) collective-permute-start(bf16[128,512]{1,0:T(8,128)(2,1)S(1)} %get-tuple-element.27), channel_id=1, source_target_pairs={{0,4},{4,0},{8,12},{12,8},{16,20},{20,16},{24,28},{28,24},{1,5},{5... | collective-permute-start | bytes 393224 | tf_op jit(solution)/shard_map/ppermute | solution.py:31
  5.5 0.1 collective-permute-start.2
  5.6 4.3 %collective-permute-done = bf16[128,512]{1,0:T(8,128)(2,1)S(1)} collective-permute-done((bf16[128,512]{1,0:T(8,128)(2,1)S(1)}, bf16[128,512]{1,0:T(8,128)(2,1)S(1)}, u32[]{:S(2)}, u32[]{:S(2)}) %collective-permute-start) | collective-permute-done | bytes 131104 | tf_op jit(solution)/shard_map/ppermute | solution.py:31
  9.8 2.1 %collective-permute-start.1 = (bf16[128,512]{1,0:T(8,128)(2,1)S(1)}, bf16[128,512]{1,0:T(8,128)(2,1)S(1)}, u32[]{:S(2)}, u32[]{:S(2)}) collective-permute-start(bf16[128,512]{1,0:T(8,128)(2,1)S(1)} %collective-permute-done), channel_id=1, source_target_pairs={{0,8},{8,16},{12,4},{16,24},{20,12},{28,20},{4,0},{24,28},{1,9},{9... | collective-permute-start | bytes 393224 | tf_op jit(solution)/shard_map/ppermute | solution.py:40
  12.0 0.7 %collective-permute-done.2 = bf16[128,512]{1,0:T(8,128)(2,1)S(1)} collective-permute-done((bf16[128,512]{1,0:T(8,128)(2,1)S(1)}, bf16[128,512]{1,0:T(8,128)(2,1)S(1)}, u32[]{:S(2)}, u32[]{:S(2)}) %collective-permute-start.2) | collective-permute-done | bytes 131104 | tf_op jit(solution)/shard_map/ppermute | solution.py:31
  12.7 1.0 %collective-permute-start.3 = (bf16[128,512]{1,0:T(8,128)(2,1)S(1)}, bf16[128,512]{1,0:T(8,128)(2,1)S(1)}, u32[]{:S(2)}, u32[]{:S(2)}) collective-permute-start(bf16[128,512]{1,0:T(8,128)(2,1)S(1)} %collective-permute-done.2), channel_id=1, source_target_pairs={{0,8},{8,16},{12,4},{16,24},{20,12},{28,20},{4,0},{24,28},{1,9},{9... | collective-permute-start | bytes 393224 | tf_op jit(solution)/shard_map/ppermute | solution.py:40
  13.7 2.2 %collective-permute-done.1 = bf16[128,512]{1,0:T(8,128)(2,1)S(1)} collective-permute-done((bf16[128,512]{1,0:T(8,128)(2,1)S(1)}, bf16[128,512]{1,0:T(8,128)(2,1)S(1)}, u32[]{:S(2)}, u32[]{:S(2)}) %collective-permute-start.1) | collective-permute-done | bytes 131104 | tf_op jit(solution)/shard_map/ppermute | solution.py:40
  16.0 1.6 %collective-permute-done.3 = bf16[128,512]{1,0:T(8,128)(2,1)S(1)} collective-permute-done((bf16[128,512]{1,0:T(8,128)(2,1)S(1)}, bf16[128,512]{1,0:T(8,128)(2,1)S(1)}, u32[]{:S(2)}, u32[]{:S(2)}) %collective-permute-start.3) | collective-permute-done | bytes 131104 | tf_op jit(solution)/shard_map/ppermute | solution.py:40
  17.6 0.1 collective-permute-start.4
  17.7 0.6 %copy-done = s32[8]{0:T(128)S(1)} copy-done((s32[8]{0:T(128)S(1)}, s32[8]{0:T(128)}, u32[]{:S(2)}) %copy-start) | copy-done | bytes 56
  18.4 4.9 %own_sum.1 = (f32[512,512]{1,0:T(8,128)S(1)}, bf16[8,512,512]{2,1,0:T(8,128)(2,1)S(1)}, bf16[8,512,512]{2,1,0:T(8,128)(2,1)S(1)}) custom-call(s32[8]{0:T(128)S(1)} %copy-done, s32[1]{0:T(128)} %copy.16.widths_in, bf16[1,512,512]{2,1,0:T(8,128)(2,1)} %state_in.1, bf16[8,1,512,512]{3,2,1,0:T(8,128)(2,1)} %left_in.1, bf16[8,1,512,512]{3,2,1,0:T(8,128)(2,1)} %right_in.1), custom_call_target="tpu_custom_call" | custom-call | flops 1431655808 | bytes 2796202 | tf_op jit(solution)/shard_map/own_sum/pallas_call | solution.py:162
  23.3 1.4 %near_sum.1.acc_in = f32[512,512]{1,0:T(8,128)S(1)} custom-call(s32[8]{0:T(128)S(1)} %copy-done, bf16[256,512]{1,0:T(8,128)(2,1)S(1)} %constant_dynamic-update-slice_fusion.2.mine, bf16[256,512]{1,0:T(8,128)(2,1)S(1)} %collective-permute-done.5.other, f32[512,512]{1,0:T(8,128)S(1)} %get-tuple-element.13.acc_in, ...), custom_call_target="tpu_custom_call" | custom-call | flops 1431655808 | bytes 2796202 | tf_op jit(solution)/shard_map/near_sum/pallas_call | solution.py:189
  24.7 2.9 %far_sum.1 = (f32[256,512]{1,0:T(8,128)S(1)}, bf16[256,512]{1,0:T(8,128)(2,1)S(1)}) custom-call(s32[8]{0:T(128)S(1)} %copy-done, bf16[256,512]{1,0:T(8,128)(2,1)S(1)} %constant_dynamic-update-slice_fusion.mine, bf16[256,512]{1,0:T(8,128)(2,1)S(1)} %collective-permute-done.4.other, f32[512,512]{1,0:T(8,128)S(1)} %near_sum.1.acc_in, ...), custom_call_target="tpu_custom_call" | custom-call | flops 1431655808 | bytes 2796202 | tf_op jit(solution)/shard_map/far_sum/pallas_call | solution.py:189
  27.6 0.6 collective-permute-start.6
  28.2 1.2 %collective-permute-done.6 = bf16[256,512]{1,0:T(8,128)(2,1)S(1)} collective-permute-done((bf16[256,512]{1,0:T(8,128)(2,1)S(1)}, bf16[256,512]{1,0:T(8,128)(2,1)S(1)}, u32[]{:S(2)}, u32[]{:S(2)}) %collective-permute-start.6) | collective-permute-done | bytes 262176 | tf_op jit(solution)/shard_map/ppermute | solution.py:26
  29.4 0.1 add_convert_fusion
  29.5 2.7 %collective-permute-start.7 = (bf16[256,512]{1,0:T(8,128)(2,1)S(1)}, bf16[256,512]{1,0:T(8,128)(2,1)S(1)}, u32[]{:S(2)}, u32[]{:S(2)}) collective-permute-start(bf16[256,512]{1,0:T(8,128)(2,1)S(1)} %add_convert_fusion), channel_id=1, source_target_pairs={{0,2},{1,3},{2,0},{3,1},{4,6},{5,7},{6,4},{7,5},{8,10},{9,11},{10,... | collective-permute-start | bytes 786440 | tf_op jit(solution)/shard_map/ppermute | solution.py:366
  32.8 6.0 %collective-permute-done.7 = bf16[256,512]{1,0:T(8,128)(2,1)S(1)} collective-permute-done((bf16[256,512]{1,0:T(8,128)(2,1)S(1)}, bf16[256,512]{1,0:T(8,128)(2,1)S(1)}, u32[]{:S(2)}, u32[]{:S(2)}) %collective-permute-start.7) | collective-permute-done | bytes 262176 | tf_op jit(solution)/shard_map/ppermute | solution.py:366
  38.7 0.2 fusion.2.mine
  39.0 1.2 %collective-permute-start.9 = (bf16[128,512]{1,0:T(8,128)(2,1)S(1)}, bf16[128,512]{1,0:T(8,128)(2,1)S(1)}, u32[]{:S(2)}, u32[]{:S(2)}) collective-permute-start(bf16[128,512]{1,0:T(8,128)(2,1)S(1)} %get-tuple-element.25), channel_id=1, source_target_pairs={{0,4},{4,0},{8,12},{12,8},{16,20},{20,16},{24,28},{28,24},{1,5},{5... | collective-permute-start | bytes 393224 | tf_op jit(solution)/shard_map/ppermute | solution.py:31
  40.2 0.9 %collective-permute-start.11 = (bf16[128,512]{1,0:T(8,128)(2,1)S(1)}, bf16[128,512]{1,0:T(8,128)(2,1)S(1)}, u32[]{:S(2)}, u32[]{:S(2)}) collective-permute-start(bf16[128,512]{1,0:T(8,128)(2,1)S(1)} %get-tuple-element.24), channel_id=1, source_target_pairs={{0,4},{4,0},{8,12},{12,8},{16,20},{20,16},{24,28},{28,24},{1,5},{5... | collective-permute-start | bytes 393224 | tf_op jit(solution)/shard_map/ppermute | solution.py:31
  41.1 4.3 %collective-permute-done.9 = bf16[128,512]{1,0:T(8,128)(2,1)S(1)} collective-permute-done((bf16[128,512]{1,0:T(8,128)(2,1)S(1)}, bf16[128,512]{1,0:T(8,128)(2,1)S(1)}, u32[]{:S(2)}, u32[]{:S(2)}) %collective-permute-start.9) | collective-permute-done | bytes 131104 | tf_op jit(solution)/shard_map/ppermute | solution.py:31
  45.5 1.2 %collective-permute-start.10 = (bf16[128,512]{1,0:T(8,128)(2,1)S(1)}, bf16[128,512]{1,0:T(8,128)(2,1)S(1)}, u32[]{:S(2)}, u32[]{:S(2)}) collective-permute-start(bf16[128,512]{1,0:T(8,128)(2,1)S(1)} %collective-permute-done.9), channel_id=1, source_target_pairs={{0,8},{8,16},{12,4},{16,24},{20,12},{28,20},{4,0},{24,28},{1,9},{9... | collective-permute-start | bytes 393224 | tf_op jit(solution)/shard_map/ppermute | solution.py:40
  46.7 1.6 %collective-permute-done.11 = bf16[128,512]{1,0:T(8,128)(2,1)S(1)} collective-permute-done((bf16[128,512]{1,0:T(8,128)(2,1)S(1)}, bf16[128,512]{1,0:T(8,128)(2,1)S(1)}, u32[]{:S(2)}, u32[]{:S(2)}) %collective-permute-start.11) | collective-permute-done | bytes 131104 | tf_op jit(solution)/shard_map/ppermute | solution.py:31
  48.3 0.1 collective-permute-start.12
  48.3 0.1 collective-permute-start.14
  48.4 2.6 %collective-permute-done.10 = bf16[128,512]{1,0:T(8,128)(2,1)S(1)} collective-permute-done((bf16[128,512]{1,0:T(8,128)(2,1)S(1)}, bf16[128,512]{1,0:T(8,128)(2,1)S(1)}, u32[]{:S(2)}, u32[]{:S(2)}) %collective-permute-start.10) | collective-permute-done | bytes 131104 | tf_op jit(solution)/shard_map/ppermute | solution.py:40
  51.1 2.1 %collective-permute-done.12 = bf16[128,512]{1,0:T(8,128)(2,1)S(1)} collective-permute-done((bf16[128,512]{1,0:T(8,128)(2,1)S(1)}, bf16[128,512]{1,0:T(8,128)(2,1)S(1)}, u32[]{:S(2)}, u32[]{:S(2)}) %collective-permute-start.12) | collective-permute-done | bytes 131104 | tf_op jit(solution)/shard_map/ppermute | solution.py:40
  53.3 5.2 %own_turn.1 = (bf16[128,512]{1,0:T(8,128)(2,1)}, bf16[8,1,512,512]{3,2,1,0:T(8,128)(2,1)}, bf16[8,512,512]{2,1,0:T(8,128)(2,1)S(1)}, bf16[512,512]{1,0:T(8,128)(2,1)S(1)}) custom-call(s32[8]{0:T(128)S(1)} %copy-done.1, bf16[256,512]{1,0:T(8,128)(2,1)S(1)} %fusion.2.mine, bf16[256,512]{1,0:T(8,128)(2,1)S(1)} %collective-permute-done.8.other, ...), custom_call_target="tpu_custom_call" | custom-call | flops 2147483648 | bytes 4194304 | tf_op jit(solution)/shard_map/own_turn/pallas_call | solution.py:269
  58.5 2.5 %near_turn.1 = (bf16[8,1,512,512]{3,2,1,0:T(8,128)(2,1)}, bf16[8,512,512]{2,1,0:T(8,128)(2,1)S(1)}) custom-call(s32[8]{0:T(128)S(1)} %copy-done.1, bf16[256,512]{1,0:T(8,128)(2,1)S(1)} %constant_dynamic-update-slice_fusion.6.mine, bf16[256,512]{1,0:T(8,128)(2,1)S(1)} %collective-permute-done.14.other, ...), custom_call_target="tpu_custom_call", output_to_operand_aliasing={{0}: (6, {})} | custom-call | flops 1431655808 | bytes 2796202 | tf_op jit(solution)/shard_map/near_turn/pallas_call | solution.py:298
  61.0 2.8 %far_turn.1 = bf16[8,1,512,512]{3,2,1,0:T(8,128)(2,1)} custom-call(s32[8]{0:T(128)S(1)} %copy-done.1, bf16[256,512]{1,0:T(8,128)(2,1)S(1)} %constant_dynamic-update-slice_fusion.4.mine, bf16[256,512]{1,0:T(8,128)(2,1)S(1)} %collective-permute-done.13.other, bf16[8,512,512]{2,1,0:T(8,128)(2,1)S(1)} %get-tuple-element.22.far_turned, ...), custom_call_target="tpu_custom_call", output_to_operand_aliasing={{}: (4, {})} | custom-call | flops 715827904 | bytes 1398101 | tf_op jit(solution)/shard_map/far_turn/pallas_call | solution.py:322
  (26 shorter events, 0.3 us)
Async XLA Ops:
  2.5 7.4 %collective-permute-start = (bf16[128,512]{1,0:T(8,128)(2,1)S(1)}, bf16[128,512]{1,0:T(8,128)(2,1)S(1)}, u32[]{:S(2)}, u32[]{:S(2)}) collective-permute-start(bf16[128,512]{1,0:T(8,128)(2,1)S(1)} %get-tuple-element.27), channel_id=1, source_target_pairs={{0,4},{4,0},{8,12},{12,8},{16,20},{20,16},{24,28},{28,24},{1,5},{5... | collective-permute-start | bytes 393224 | tf_op jit(solution)/shard_map/ppermute | solution.py:31
  5.5 7.2 %collective-permute-start.2 = (bf16[128,512]{1,0:T(8,128)(2,1)S(1)}, bf16[128,512]{1,0:T(8,128)(2,1)S(1)}, u32[]{:S(2)}, u32[]{:S(2)}) collective-permute-start(bf16[128,512]{1,0:T(8,128)(2,1)S(1)} %get-tuple-element.26), channel_id=1, source_target_pairs={{0,4},{4,0},{8,12},{12,8},{16,20},{20,16},{24,28},{28,24},{1,5},{5... | collective-permute-start | bytes 393224 | tf_op jit(solution)/shard_map/ppermute | solution.py:31
  9.8 6.1 %collective-permute-start.1 = (bf16[128,512]{1,0:T(8,128)(2,1)S(1)}, bf16[128,512]{1,0:T(8,128)(2,1)S(1)}, u32[]{:S(2)}, u32[]{:S(2)}) collective-permute-start(bf16[128,512]{1,0:T(8,128)(2,1)S(1)} %collective-permute-done), channel_id=1, source_target_pairs={{0,8},{8,16},{12,4},{16,24},{20,12},{28,20},{4,0},{24,28},{1,9},{9... | collective-permute-start | bytes 393224 | tf_op jit(solution)/shard_map/ppermute | solution.py:40
  12.7 5.0 %collective-permute-start.3 = (bf16[128,512]{1,0:T(8,128)(2,1)S(1)}, bf16[128,512]{1,0:T(8,128)(2,1)S(1)}, u32[]{:S(2)}, u32[]{:S(2)}) collective-permute-start(bf16[128,512]{1,0:T(8,128)(2,1)S(1)} %collective-permute-done.2), channel_id=1, source_target_pairs={{0,8},{8,16},{12,4},{16,24},{20,12},{28,20},{4,0},{24,28},{1,9},{9... | collective-permute-start | bytes 393224 | tf_op jit(solution)/shard_map/ppermute | solution.py:40
  13.6 9.7 %collective-permute-start.5 = (bf16[256,512]{1,0:T(8,128)(2,1)S(1)}, bf16[256,512]{1,0:T(8,128)(2,1)S(1)}, u32[]{:S(2)}, u32[]{:S(2)}) collective-permute-start(bf16[256,512]{1,0:T(8,128)(2,1)S(1)} %constant_dynamic-update-slice_fusion.2.mine), channel_id=1, source_target_pairs={{0,1},{1,0},{2,3},{3,2},{4,5},{5,4},{6,7},{7,6},{8,9},{9,8},{10,11... | collective-permute-start | bytes 786440 | tf_op jit(solution)/shard_map/ppermute | solution.py:26
  17.6 7.1 %collective-permute-start.4 = (bf16[256,512]{1,0:T(8,128)(2,1)S(1)}, bf16[256,512]{1,0:T(8,128)(2,1)S(1)}, u32[]{:S(2)}, u32[]{:S(2)}) collective-permute-start(bf16[256,512]{1,0:T(8,128)(2,1)S(1)} %constant_dynamic-update-slice_fusion.mine), channel_id=1, source_target_pairs={{0,1},{1,0},{2,3},{3,2},{4,5},{5,4},{6,7},{7,6},{8,9},{9,8},{10,11... | collective-permute-start | bytes 786440 | tf_op jit(solution)/shard_map/ppermute | solution.py:26
  17.7 0.7 %copy-start = (s32[8]{0:T(128)S(1)}, s32[8]{0:T(128)}, u32[]{:S(2)}) copy-start(s32[8]{0:T(128)} %shifts.9) | copy-start | bytes 100
  24.7 14.1 %copy-start.2 = (bf16[1,512,512]{2,1,0:T(8,128)(2,1)S(1)}, bf16[1,512,512]{2,1,0:T(8,128)(2,1)}, u32[]{:S(2)}) copy-start(bf16[1,512,512]{2,1,0:T(8,128)(2,1)} %state_in.1) | copy-start | bytes 1572868
  24.7 28.6 %copy-start.1 = (s32[8]{0:T(128)S(1)}, s32[8]{0:T(128)}, u32[]{:S(2)}) copy-start(s32[8]{0:T(128)} %shifts.9) | copy-start | bytes 100
  27.6 1.7 %collective-permute-start.6 = (bf16[256,512]{1,0:T(8,128)(2,1)S(1)}, bf16[256,512]{1,0:T(8,128)(2,1)S(1)}, u32[]{:S(2)}, u32[]{:S(2)}) collective-permute-start(bf16[256,512]{1,0:T(8,128)(2,1)S(1)} %get-tuple-element.17), channel_id=1, source_target_pairs={{0,1},{1,0},{2,3},{3,2},{4,5},{5,4},{6,7},{7,6},{8,9},{9,8},{10,11... | collective-permute-start | bytes 786440 | tf_op jit(solution)/shard_map/ppermute | solution.py:26
  29.5 9.3 %collective-permute-start.7 = (bf16[256,512]{1,0:T(8,128)(2,1)S(1)}, bf16[256,512]{1,0:T(8,128)(2,1)S(1)}, u32[]{:S(2)}, u32[]{:S(2)}) collective-permute-start(bf16[256,512]{1,0:T(8,128)(2,1)S(1)} %add_convert_fusion), channel_id=1, source_target_pairs={{0,2},{1,3},{2,0},{3,1},{4,6},{5,7},{6,4},{7,5},{8,10},{9,11},{10,... | collective-permute-start | bytes 786440 | tf_op jit(solution)/shard_map/ppermute | solution.py:366
  39.0 6.4 %collective-permute-start.9 = (bf16[128,512]{1,0:T(8,128)(2,1)S(1)}, bf16[128,512]{1,0:T(8,128)(2,1)S(1)}, u32[]{:S(2)}, u32[]{:S(2)}) collective-permute-start(bf16[128,512]{1,0:T(8,128)(2,1)S(1)} %get-tuple-element.25), channel_id=1, source_target_pairs={{0,4},{4,0},{8,12},{12,8},{16,20},{20,16},{24,28},{28,24},{1,5},{5... | collective-permute-start | bytes 393224 | tf_op jit(solution)/shard_map/ppermute | solution.py:31
  40.2 8.0 %collective-permute-start.11 = (bf16[128,512]{1,0:T(8,128)(2,1)S(1)}, bf16[128,512]{1,0:T(8,128)(2,1)S(1)}, u32[]{:S(2)}, u32[]{:S(2)}) collective-permute-start(bf16[128,512]{1,0:T(8,128)(2,1)S(1)} %get-tuple-element.24), channel_id=1, source_target_pairs={{0,4},{4,0},{8,12},{12,8},{16,20},{20,16},{24,28},{28,24},{1,5},{5... | collective-permute-start | bytes 393224 | tf_op jit(solution)/shard_map/ppermute | solution.py:31
  41.1 12.2 %collective-permute-start.8 = (bf16[256,512]{1,0:T(8,128)(2,1)S(1)}, bf16[256,512]{1,0:T(8,128)(2,1)S(1)}, u32[]{:S(2)}, u32[]{:S(2)}) collective-permute-start(bf16[256,512]{1,0:T(8,128)(2,1)S(1)} %fusion.2.mine), channel_id=1, source_target_pairs={{0,1},{1,0},{2,3},{3,2},{4,5},{5,4},{6,7},{7,6},{8,9},{9,8},{10,11... | collective-permute-start | bytes 786440 | tf_op jit(solution)/shard_map/ppermute | solution.py:26
  45.5 5.6 %collective-permute-start.10 = (bf16[128,512]{1,0:T(8,128)(2,1)S(1)}, bf16[128,512]{1,0:T(8,128)(2,1)S(1)}, u32[]{:S(2)}, u32[]{:S(2)}) collective-permute-start(bf16[128,512]{1,0:T(8,128)(2,1)S(1)} %collective-permute-done.9), channel_id=1, source_target_pairs={{0,8},{8,16},{12,4},{16,24},{20,12},{28,20},{4,0},{24,28},{1,9},{9... | collective-permute-start | bytes 393224 | tf_op jit(solution)/shard_map/ppermute | solution.py:40
  48.3 5.0 %collective-permute-start.12 = (bf16[128,512]{1,0:T(8,128)(2,1)S(1)}, bf16[128,512]{1,0:T(8,128)(2,1)S(1)}, u32[]{:S(2)}, u32[]{:S(2)}) collective-permute-start(bf16[128,512]{1,0:T(8,128)(2,1)S(1)} %collective-permute-done.11), channel_id=1, source_target_pairs={{0,8},{8,16},{12,4},{16,24},{20,12},{28,20},{4,0},{24,28},{1,9},{9... | collective-permute-start | bytes 393224 | tf_op jit(solution)/shard_map/ppermute | solution.py:40
  48.3 10.2 %collective-permute-start.14 = (bf16[256,512]{1,0:T(8,128)(2,1)S(1)}, bf16[256,512]{1,0:T(8,128)(2,1)S(1)}, u32[]{:S(2)}, u32[]{:S(2)}) collective-permute-start(bf16[256,512]{1,0:T(8,128)(2,1)S(1)} %constant_dynamic-update-slice_fusion.6.mine), channel_id=1, source_target_pairs={{0,1},{1,0},{2,3},{3,2},{4,5},{5,4},{6,7},{7,6},{8,9},{9,8},{10,11... | collective-permute-start | bytes 786440 | tf_op jit(solution)/shard_map/ppermute | solution.py:26
  53.2 7.8 %collective-permute-start.13 = (bf16[256,512]{1,0:T(8,128)(2,1)S(1)}, bf16[256,512]{1,0:T(8,128)(2,1)S(1)}, u32[]{:S(2)}, u32[]{:S(2)}) collective-permute-start(bf16[256,512]{1,0:T(8,128)(2,1)S(1)} %constant_dynamic-update-slice_fusion.4.mine), channel_id=1, source_target_pairs={{0,1},{1,0},{2,3},{3,2},{4,5},{5,4},{6,7},{7,6},{8,9},{9,8},{10,11... | collective-permute-start | bytes 786440 | tf_op jit(solution)/shard_map/ppermute | solution.py:26

commit v3 on v2

--- a/solution.py
+++ b/solution.py
@@ -71,22 +71,41 @@
             dst[...] = jnp.zeros_like(dst)
 
 
+def by_twos(first, count, step):
+    pairs = lax.div(count - first, 2)
+
+    def body(i, carry):
+        step(first + 2 * i, 2)
+        return carry
+
+    lax.fori_loop(0, pairs, body, 0)
+
+    @pl.when(count - first > 2 * pairs)
+    def _():
+        step(count - 1, 1)
+
+
 def add_terms(count, order, src, left, right, acc, ready):
-    def body(i, carry):
-        channel = order[i]
-        ready(channel)
-        halfway = jnp.dot(left[channel], src[...], preferred_element_type=F32).astype(BF16)
-        acc[...] += lax.dot_general(
-            halfway, right[channel], (((1,), (1,)), ((), ())), preferred_element_type=F32
-        )
-        return carry
-
-    lax.fori_loop(0, count, body, 0)
+    def step(i, n):
+        channels = [order[i + j] for j in range(n)]
+        for channel in channels:
+            ready(channel)
+        halfway = [
+            jnp.dot(left[channel], src[...], preferred_element_type=F32).astype(BF16)
+            for channel in channels
+        ]
+        terms = [
+            lax.dot_general(h, right[channel], (((1,), (1,)), ((), ())), preferred_element_type=F32)
+            for h, channel in zip(halfway, channels)
+        ]
+        acc[...] += sum(terms[1:], terms[0])
+
+    by_twos(0, count, step)
 
 
 def own_sum_kernel(
-    shifts_in, widths_in, state_in, left_in, right_in, acc, left, right,
-    src, shifts, widths, order, small_sem, left_sem, right_sem
+    shifts_in, widths_in, state_in, left_in, right_in, acc, left, right, shifts,
+    src, widths, order, small_sem, left_sem, right_sem
 ):
     small = [
         pltpu.make_async_copy(shifts_in, shifts, small_sem.at[0]),
@@ -162,11 +181,15 @@
     return pl.pallas_call(
         own_sum_kernel,
         in_specs=[ANY] * 5,
-        out_specs=[VMEM] * 3,
-        out_shape=[jax.ShapeDtypeStruct((pad, pad), F32), blocks, blocks],
+        out_specs=[VMEM] * 3 + [SMEM],
+        out_shape=[
+            jax.ShapeDtypeStruct((pad, pad), F32),
+            blocks,
+            blocks,
+            jax.ShapeDtypeStruct(shifts.shape, jnp.int32),
+        ],
         scratch_shapes=[
             pltpu.VMEM((pad, pad), BF16),
-            pltpu.SMEM(shifts.shape, jnp.int32),
             pltpu.SMEM(widths.shape, jnp.int32),
             pltpu.SMEM((chans + 1,), jnp.int32),
             pltpu.SemaphoreType.DMA((3,)),
@@ -209,14 +232,15 @@
     def store(i):
         return pltpu.make_async_copy(obuf.at[i], new_left.at[order[i], 0], osem.at[i])
 
-    def body(i, carry):
-        bra_left = ready[i] if turned is None else turned(order[i])
-        rotated = jnp.dot(bra_left, src[...], preferred_element_type=F32)
-        obuf[i] = (rotated * scale).astype(BF16)
-        store(i).start()
-        return carry
-
-    lax.fori_loop(first, count, body, 0)
+    def step(i, n):
+        slots = [i + j for j in range(n)]
+        bra_left = [ready[k] if turned is None else turned(order[k]) for k in slots]
+        rotated = [jnp.dot(x, src[...], preferred_element_type=F32) for x in bra_left]
+        for k, x in zip(slots, rotated):
+            obuf[k] = (x * scale).astype(BF16)
+            store(k).start()
+
+    by_twos(first, count, step)
 
     def drain(i, carry):
         store(i).wait()
@@ -232,11 +256,11 @@
 def turn_ahead(shifts, order, wanted, bra, left, half_turned):
     count = list_channels(shifts, order, wanted)
 
-    def body(i, carry):
-        half_turned[i] = turn(bra, left, order[i])
-        return carry
-
-    lax.fori_loop(0, count, body, 0)
+    def step(i, n):
+        for k, x in [(i + j, turn(bra, left, order[i + j])) for j in range(n)]:
+            half_turned[k] = x
+
+    by_twos(0, count, step)
 
 
 def own_turn_kernel(
@@ -332,13 +356,15 @@
     )(shifts, held(mine), held(other), held(far_turned), new_left)
 
 
-def exchange(mine):
-    near_a = swap_near(mine[: mine.shape[0] // 2])
-    near_b = swap_near(mine[mine.shape[0] // 2 :])
-    far_a = pass_far(near_a)
-    far_b = pass_far(near_b)
-    near = held(jnp.concatenate([near_a, near_b]))
-    far = held(jnp.concatenate([far_a, far_b]))
+def exchange(mine, chunks):
+    rows = mine.shape[0] // chunks
+    near, far = [], []
+    for i in range(chunks):
+        near.append(swap_near(mine[i * rows : (i + 1) * rows]))
+    for i in range(chunks):
+        far.append(pass_far(near[i]))
+    near = held(jnp.concatenate(near))
+    far = held(jnp.concatenate(far))
     near_other = swap_core(near)
     far_other = swap_core(far)
     return near, near_other, far, far_other
@@ -355,8 +381,8 @@
     state_m = lax.dynamic_slice_in_dim(state_blocks[0], first, half, 0)
     state_m = jnp.where(inside, state_m, jnp.zeros_like(state_m))
 
-    near_m, near_o, far_m, far_o = exchange(state_m)
-    acc, left, right = own_sum(shifts, widths, state_blocks, left_blocks, right_blocks)
+    near_m, near_o, far_m, far_o = exchange(state_m, 2)
+    acc, left, right, shifts = own_sum(shifts, widths, state_blocks, left_blocks, right_blocks)
     acc = next_sum(NEAR, False, shifts, near_m, near_o, acc, left, right)
     keep, give = next_sum(FAR, True, shifts, far_m, far_o, acc, left, right)
 
@@ -371,7 +397,7 @@
     corrected = state_m.astype(F32) - step_sizes[0] * product
     update_m = jnp.where(inside, corrected, jnp.zeros_like(corrected)).astype(BF16)
 
-    near_m, near_o, far_m, far_o = exchange(update_m)
+    near_m, near_o, far_m, far_o = exchange(update_m, 1)
     update_o = swap_core(update_m)
     rows, new_left, half_turned, bra = own_turn(shifts, update_m, update_o, left, pad // chan_count)
     new_left, far_turned = near_turn(

time: 64 us -> 63.9 us (level)
  waiting for transfers between devices: 26.7 us -> 27.4 us
    ppermute x4 -> x3, starting transfers between devices: 5.2 us -> 4.52 us  [swap_near(): lax.ppermute(x, 'sec', [(i, i ^ 1) for i in range(count) if i ^ 1 < count])]
    ppermute x4 -> x3, waiting for transfers between devices: 10.9 us -> 11.4 us  [swap_near(): lax.ppermute(x, 'sec', [(i, i ^ 1) for i in range(count) if i ^ 1 < count])]
    ppermute x4 -> x3, waiting for transfers between devices: 8.67 us -> 8.91 us  [pass_far(): return lax.ppermute(x, 'sec', pairs + list(zip(sources, targets)))]
    ppermute x4 -> x3, starting transfers between devices: 4.39 us -> 4.47 us  [pass_far(): return lax.ppermute(x, 'sec', pairs + list(zip(sources, targets)))]
  transfers between devices with their start and end apart: 15 -> 13, of which waited for: 10 -> 8; matrix products, arithmetic and copies ran while one was open for 0% -> 0% of each run, Pallas kernels for 22% -> 22%
where the time goes in v3:
time: 63.9 us; the launch traced here: 63.7 us
  waiting for transfers between devices  27.4 us (43%)
  Pallas kernels  19.4 us (30%)
  starting transfers between devices  12.6 us (20%)
  between operations  2.12 us (3%)
  other arithmetic  1.42 us (2%)
  local copies, waits for them, and re-layouts  0.72 us (1%)
    ppermute x3, waiting for transfers between devices, swap_near(): lax.ppermute(x, 'sec', [(i, i ^ 1) for i in range(count) if i ^ 1 < count])  11.4 us
    ppermute x3, waiting for transfers between devices, pass_far(): return lax.ppermute(x, 'sec', pairs + list(zip(sources, targets)))  8.91 us
    ppermute x1, waiting for transfers between devices, body(): lax.ppermute(pair_sum, 'chan', [(i, (i + turn) % chan_count) for i in ran...  5.96 us
    pallas_call x1, Pallas kernels, own_sum(): pl.pallas_call(own_sum_kernel, in_specs=[ANY] * 5, out_specs=[VMEM] * 3 +...  5.48 us
    pallas_call x1, Pallas kernels, own_turn(): pl.pallas_call(own_turn_kernel, in_specs=[SMEM, VMEM, VMEM, VMEM], out_sp...  4.81 us
    ppermute x3, starting transfers between devices, swap_near(): lax.ppermute(x, 'sec', [(i, i ^ 1) for i in range(count) if i ^ 1 < count])  4.52 us
    ppermute x3, starting transfers between devices, pass_far(): return lax.ppermute(x, 'sec', pairs + list(zip(sources, targets)))  4.47 us
    pallas_call x2, Pallas kernels, next_sum(): pl.pallas_call(functools.partial(next_sum_kernel, wanted, last), in_specs...  4.13 us
  transfers between devices with their start and end apart: 13, of which 8 were waited for; matrix products, arithmetic and copies ran while one was open for 0% of the time, Pallas kernels for 22%

profile of v3, /device:TPU:0, one launch (start us, length us, event | category | flops | bytes accessed | tf_op | source)
XLA Modules:
  0.0 63.7 jit_solution(14421032765716931179)
XLA Ops:
  1.3 1.1 %and_select_fusion.2 = bf16[256,512]{1,0:T(8,128)(2,1)S(1)} fusion(bf16[1,512,512]{2,1,0:T(8,128)(2,1)} %state_in.1, s32[]{:T(128)S(6)} %select_n.22, pred[512]{0:T(512)(128)(4,1)S(1)} %iota_compare_fusion, pred[256]{0:T(512)(128)(4,1)S(1)} %add_compare_fusion), kind=kLoop, calls=%fused_computation.2 | loop fusion | flops 262144 | bytes 525060 | tf_op jit(solution)/shard_map/jit(_where)/select_n | solution.py:382
  2.5 3.0 %collective-permute-start = (bf16[128,512]{1,0:T(8,128)(2,1)S(1)}, bf16[128,512]{1,0:T(8,128)(2,1)S(1)}, u32[]{:S(2)}, u32[]{:S(2)}) collective-permute-start(bf16[128,512]{1,0:T(8,128)(2,1)S(1)} %get-tuple-element.27), channel_id=1, source_target_pairs={{0,4},{4,0},{8,12},{12,8},{16,20},{20,16},{24,28},{28,24},{1,5},{5... | collective-permute-start | bytes 393224 | tf_op jit(solution)/shard_map/ppermute | solution.py:31
  5.5 0.1 collective-permute-start.2
  5.6 4.3 %collective-permute-done = bf16[128,512]{1,0:T(8,128)(2,1)S(1)} collective-permute-done((bf16[128,512]{1,0:T(8,128)(2,1)S(1)}, bf16[128,512]{1,0:T(8,128)(2,1)S(1)}, u32[]{:S(2)}, u32[]{:S(2)}) %collective-permute-start) | collective-permute-done | bytes 131104 | tf_op jit(solution)/shard_map/ppermute | solution.py:31
  9.8 2.1 %collective-permute-start.1 = (bf16[128,512]{1,0:T(8,128)(2,1)S(1)}, bf16[128,512]{1,0:T(8,128)(2,1)S(1)}, u32[]{:S(2)}, u32[]{:S(2)}) collective-permute-start(bf16[128,512]{1,0:T(8,128)(2,1)S(1)} %collective-permute-done), channel_id=1, source_target_pairs={{0,8},{8,16},{12,4},{16,24},{20,12},{28,20},{4,0},{24,28},{1,9},{9... | collective-permute-start | bytes 393224 | tf_op jit(solution)/shard_map/ppermute | solution.py:40
  12.0 0.7 %collective-permute-done.2 = bf16[128,512]{1,0:T(8,128)(2,1)S(1)} collective-permute-done((bf16[128,512]{1,0:T(8,128)(2,1)S(1)}, bf16[128,512]{1,0:T(8,128)(2,1)S(1)}, u32[]{:S(2)}, u32[]{:S(2)}) %collective-permute-start.2) | collective-permute-done | bytes 131104 | tf_op jit(solution)/shard_map/ppermute | solution.py:31
  12.7 1.0 %collective-permute-start.3 = (bf16[128,512]{1,0:T(8,128)(2,1)S(1)}, bf16[128,512]{1,0:T(8,128)(2,1)S(1)}, u32[]{:S(2)}, u32[]{:S(2)}) collective-permute-start(bf16[128,512]{1,0:T(8,128)(2,1)S(1)} %collective-permute-done.2), channel_id=1, source_target_pairs={{0,8},{8,16},{12,4},{16,24},{20,12},{28,20},{4,0},{24,28},{1,9},{9... | collective-permute-start | bytes 393224 | tf_op jit(solution)/shard_map/ppermute | solution.py:40
  13.6 0.1 collective-permute-start.5
  13.7 2.2 %collective-permute-done.1 = bf16[128,512]{1,0:T(8,128)(2,1)S(1)} collective-permute-done((bf16[128,512]{1,0:T(8,128)(2,1)S(1)}, bf16[128,512]{1,0:T(8,128)(2,1)S(1)}, u32[]{:S(2)}, u32[]{:S(2)}) %collective-permute-start.1) | collective-permute-done | bytes 131104 | tf_op jit(solution)/shard_map/ppermute | solution.py:40
  16.0 1.6 %collective-permute-done.3 = bf16[128,512]{1,0:T(8,128)(2,1)S(1)} collective-permute-done((bf16[128,512]{1,0:T(8,128)(2,1)S(1)}, bf16[128,512]{1,0:T(8,128)(2,1)S(1)}, u32[]{:S(2)}, u32[]{:S(2)}) %collective-permute-start.3) | collective-permute-done | bytes 131104 | tf_op jit(solution)/shard_map/ppermute | solution.py:40
  17.6 0.1 collective-permute-start.4
  17.7 0.0 copy-start
  17.7 0.6 %copy-done = s32[8]{0:T(128)S(1)} copy-done((s32[8]{0:T(128)S(1)}, s32[8]{0:T(128)}, u32[]{:S(2)}) %copy-start) | copy-done | bytes 56
  18.4 5.5 %own_sum.1 = (f32[512,512]{1,0:T(8,128)S(1)}, bf16[8,512,512]{2,1,0:T(8,128)(2,1)S(1)}, bf16[8,512,512]{2,1,0:T(8,128)(2,1)S(1)}, s32[8]{0:T(128)S(1)}) custom-call(s32[8]{0:T(128)S(1)} %copy-done, s32[1]{0:T(128)} %copy.14.widths_in, bf16[1,512,512]{2,1,0:T(8,128)(2,1)} %state_in.1, bf16[8,1,512,512]{3,2,1,0:T(8,128)(2,1)} %left_in.1, ...), custom_call_target="tpu_custom_call" | custom-call | flops 1431655808 | bytes 2796202 | tf_op jit(solution)/shard_map/own_sum/pallas_call | solution.py:181
  23.9 0.0 collective-permute-done.5.other
  23.9 1.4 %near_sum.1.acc_in = f32[512,512]{1,0:T(8,128)S(1)} custom-call(s32[8]{0:T(128)S(1)} %get-tuple-element.14.shifts, bf16[256,512]{1,0:T(8,128)(2,1)S(1)} %constant_dynamic-update-slice_fusion.2.mine, bf16[256,512]{1,0:T(8,128)(2,1)S(1)} %collective-permute-done.5.other, f32[512,512]{1,0:T(8,128)S(1)} %get-tuple-element.15.acc_in, ...), custom_call_target="tpu_custom_call" | custom-call | flops 1431655808 | bytes 2796202 | tf_op jit(solution)/shard_map/near_sum/pallas_call | solution.py:212
  25.3 0.0 copy-start.1
  25.3 2.7 %far_sum.1 = (f32[256,512]{1,0:T(8,128)S(1)}, bf16[256,512]{1,0:T(8,128)(2,1)S(1)}) custom-call(s32[8]{0:T(128)S(1)} %get-tuple-element.14.shifts, bf16[256,512]{1,0:T(8,128)(2,1)S(1)} %constant_dynamic-update-slice_fusion.mine, bf16[256,512]{1,0:T(8,128)(2,1)S(1)} %collective-permute-done.4.other, f32[512,512]{1,0:T(8,128)S(1)} %near_sum.1.acc_in, ...), custom_call_target="tpu_custom_call" | custom-call | flops 1431655808 | bytes 2796202 | tf_op jit(solution)/shard_map/far_sum/pallas_call | solution.py:212
  28.0 0.6 collective-permute-start.6
  28.6 1.2 %collective-permute-done.6 = bf16[256,512]{1,0:T(8,128)(2,1)S(1)} collective-permute-done((bf16[256,512]{1,0:T(8,128)(2,1)S(1)}, bf16[256,512]{1,0:T(8,128)(2,1)S(1)}, u32[]{:S(2)}, u32[]{:S(2)}) %collective-permute-start.6) | collective-permute-done | bytes 262176 | tf_op jit(solution)/shard_map/ppermute | solution.py:26
  29.8 0.1 add_convert_fusion
  29.8 2.4 %collective-permute-start.7 = (bf16[256,512]{1,0:T(8,128)(2,1)S(1)}, bf16[256,512]{1,0:T(8,128)(2,1)S(1)}, u32[]{:S(2)}, u32[]{:S(2)}) collective-permute-start(bf16[256,512]{1,0:T(8,128)(2,1)S(1)} %add_convert_fusion), channel_id=1, source_target_pairs={{0,2},{1,3},{2,0},{3,1},{4,6},{5,7},{6,4},{7,5},{8,10},{9,11},{10,... | collective-permute-start | bytes 786440 | tf_op jit(solution)/shard_map/ppermute | solution.py:392
  32.9 6.0 %collective-permute-done.7 = bf16[256,512]{1,0:T(8,128)(2,1)S(1)} collective-permute-done((bf16[256,512]{1,0:T(8,128)(2,1)S(1)}, bf16[256,512]{1,0:T(8,128)(2,1)S(1)}, u32[]{:S(2)}, u32[]{:S(2)}) %collective-permute-start.7) | collective-permute-done | bytes 262176 | tf_op jit(solution)/shard_map/ppermute | solution.py:392
  38.8 0.2 fusion.2.mine
  39.1 1.4 %collective-permute-start.9 = (bf16[256,512]{1,0:T(8,128)(2,1)S(1)}, bf16[256,512]{1,0:T(8,128)(2,1)S(1)}, u32[]{:S(2)}, u32[]{:S(2)}) collective-permute-start(bf16[256,512]{1,0:T(8,128)(2,1)S(1)} %fusion.2.mine), channel_id=1, source_target_pairs={{0,4},{4,0},{8,12},{12,8},{16,20},{20,16},{24,28},{28,24},{1,5},{5... | collective-permute-start | bytes 786440 | tf_op jit(solution)/shard_map/ppermute | solution.py:31
  40.5 6.4 %collective-permute-done.9.mine = bf16[256,512]{1,0:T(8,128)(2,1)S(1)} collective-permute-done((bf16[256,512]{1,0:T(8,128)(2,1)S(1)}, bf16[256,512]{1,0:T(8,128)(2,1)S(1)}, u32[]{:S(2)}, u32[]{:S(2)}) %collective-permute-start.9) | collective-permute-done | bytes 262176 | tf_op jit(solution)/shard_map/ppermute | solution.py:31
  46.9 1.4 %collective-permute-start.10 = (bf16[256,512]{1,0:T(8,128)(2,1)S(1)}, bf16[256,512]{1,0:T(8,128)(2,1)S(1)}, u32[]{:S(2)}, u32[]{:S(2)}) collective-permute-start(bf16[256,512]{1,0:T(8,128)(2,1)S(1)} %collective-permute-done.9.mine), channel_id=1, source_target_pairs={{0,8},{8,16},{12,4},{16,24},{20,12},{28,20},{4,0},{24,28},{1,9},{9... | collective-permute-start | bytes 786440 | tf_op jit(solution)/shard_map/ppermute | solution.py:40
  48.3 0.5 collective-permute-start.12
  48.8 5.0 %collective-permute-done.10.mine = bf16[256,512]{1,0:T(8,128)(2,1)S(1)} collective-permute-done((bf16[256,512]{1,0:T(8,128)(2,1)S(1)}, bf16[256,512]{1,0:T(8,128)(2,1)S(1)}, u32[]{:S(2)}, u32[]{:S(2)}) %collective-permute-start.10) | collective-permute-done | bytes 262176 | tf_op jit(solution)/shard_map/ppermute | solution.py:40
  53.8 4.8 %own_turn.1 = (bf16[128,512]{1,0:T(8,128)(2,1)}, bf16[8,1,512,512]{3,2,1,0:T(8,128)(2,1)}, bf16[8,512,512]{2,1,0:T(8,128)(2,1)S(1)}, bf16[512,512]{1,0:T(8,128)(2,1)S(1)}) custom-call(s32[8]{0:T(128)S(1)} %get-tuple-element.14.shifts, bf16[256,512]{1,0:T(8,128)(2,1)S(1)} %fusion.2.mine, bf16[256,512]{1,0:T(8,128)(2,1)S(1)} %collective-permute-done.8.other, ...), custom_call_target="tpu_custom_call" | custom-call | flops 2147483648 | bytes 4194304 | tf_op jit(solution)/shard_map/own_turn/pallas_call | solution.py:293
  58.7 2.3 %near_turn.1 = (bf16[8,1,512,512]{3,2,1,0:T(8,128)(2,1)}, bf16[8,512,512]{2,1,0:T(8,128)(2,1)S(1)}) custom-call(s32[8]{0:T(128)S(1)} %get-tuple-element.14.shifts, bf16[256,512]{1,0:T(8,128)(2,1)S(1)} %collective-permute-done.9.mine, bf16[256,512]{1,0:T(8,128)(2,1)S(1)} %collective-permute-done.12.other, ...), custom_call_target="tpu_custom_call", output_to_operand_aliasing={{0}: (6, {})} | custom-call | flops 1431655808 | bytes 2796202 | tf_op jit(solution)/shard_map/near_turn/pallas_call | solution.py:322
  61.0 2.7 %far_turn.1 = bf16[8,1,512,512]{3,2,1,0:T(8,128)(2,1)} custom-call(s32[8]{0:T(128)S(1)} %get-tuple-element.14.shifts, bf16[256,512]{1,0:T(8,128)(2,1)S(1)} %collective-permute-done.10.mine, bf16[256,512]{1,0:T(8,128)(2,1)S(1)} %collective-permute-done.11.other, ...), custom_call_target="tpu_custom_call", output_to_operand_aliasing={{}: (4, {})} | custom-call | flops 715827904 | bytes 1398101 | tf_op jit(solution)/shard_map/far_turn/pallas_call | solution.py:346
  (15 shorter events, 0.1 us)
Async XLA Ops:
  2.5 7.4 %collective-permute-start = (bf16[128,512]{1,0:T(8,128)(2,1)S(1)}, bf16[128,512]{1,0:T(8,128)(2,1)S(1)}, u32[]{:S(2)}, u32[]{:S(2)}) collective-permute-start(bf16[128,512]{1,0:T(8,128)(2,1)S(1)} %get-tuple-element.27), channel_id=1, source_target_pairs={{0,4},{4,0},{8,12},{12,8},{16,20},{20,16},{24,28},{28,24},{1,5},{5... | collective-permute-start | bytes 393224 | tf_op jit(solution)/shard_map/ppermute | solution.py:31
  5.5 7.2 %collective-permute-start.2 = (bf16[128,512]{1,0:T(8,128)(2,1)S(1)}, bf16[128,512]{1,0:T(8,128)(2,1)S(1)}, u32[]{:S(2)}, u32[]{:S(2)}) collective-permute-start(bf16[128,512]{1,0:T(8,128)(2,1)S(1)} %get-tuple-element.26), channel_id=1, source_target_pairs={{0,4},{4,0},{8,12},{12,8},{16,20},{20,16},{24,28},{28,24},{1,5},{5... | collective-permute-start | bytes 393224 | tf_op jit(solution)/shard_map/ppermute | solution.py:31
  9.8 6.1 %collective-permute-start.1 = (bf16[128,512]{1,0:T(8,128)(2,1)S(1)}, bf16[128,512]{1,0:T(8,128)(2,1)S(1)}, u32[]{:S(2)}, u32[]{:S(2)}) collective-permute-start(bf16[128,512]{1,0:T(8,128)(2,1)S(1)} %collective-permute-done), channel_id=1, source_target_pairs={{0,8},{8,16},{12,4},{16,24},{20,12},{28,20},{4,0},{24,28},{1,9},{9... | collective-permute-start | bytes 393224 | tf_op jit(solution)/shard_map/ppermute | solution.py:40
  12.7 5.0 %collective-permute-start.3 = (bf16[128,512]{1,0:T(8,128)(2,1)S(1)}, bf16[128,512]{1,0:T(8,128)(2,1)S(1)}, u32[]{:S(2)}, u32[]{:S(2)}) collective-permute-start(bf16[128,512]{1,0:T(8,128)(2,1)S(1)} %collective-permute-done.2), channel_id=1, source_target_pairs={{0,8},{8,16},{12,4},{16,24},{20,12},{28,20},{4,0},{24,28},{1,9},{9... | collective-permute-start | bytes 393224 | tf_op jit(solution)/shard_map/ppermute | solution.py:40
  13.6 10.2 %collective-permute-start.5 = (bf16[256,512]{1,0:T(8,128)(2,1)S(1)}, bf16[256,512]{1,0:T(8,128)(2,1)S(1)}, u32[]{:S(2)}, u32[]{:S(2)}) collective-permute-start(bf16[256,512]{1,0:T(8,128)(2,1)S(1)} %constant_dynamic-update-slice_fusion.2.mine), channel_id=1, source_target_pairs={{0,1},{1,0},{2,3},{3,2},{4,5},{5,4},{6,7},{7,6},{8,9},{9,8},{10,11... | collective-permute-start | bytes 786440 | tf_op jit(solution)/shard_map/ppermute | solution.py:26
  17.6 7.6 %collective-permute-start.4 = (bf16[256,512]{1,0:T(8,128)(2,1)S(1)}, bf16[256,512]{1,0:T(8,128)(2,1)S(1)}, u32[]{:S(2)}, u32[]{:S(2)}) collective-permute-start(bf16[256,512]{1,0:T(8,128)(2,1)S(1)} %constant_dynamic-update-slice_fusion.mine), channel_id=1, source_target_pairs={{0,1},{1,0},{2,3},{3,2},{4,5},{5,4},{6,7},{7,6},{8,9},{9,8},{10,11... | collective-permute-start | bytes 786440 | tf_op jit(solution)/shard_map/ppermute | solution.py:26
  17.7 0.7 %copy-start = (s32[8]{0:T(128)S(1)}, s32[8]{0:T(128)}, u32[]{:S(2)}) copy-start(s32[8]{0:T(128)} %shifts_in.1) | copy-start | bytes 100
  25.3 13.6 %copy-start.1 = (bf16[1,512,512]{2,1,0:T(8,128)(2,1)S(1)}, bf16[1,512,512]{2,1,0:T(8,128)(2,1)}, u32[]{:S(2)}) copy-start(bf16[1,512,512]{2,1,0:T(8,128)(2,1)} %state_in.1) | copy-start | bytes 1572868
  28.0 1.7 %collective-permute-start.6 = (bf16[256,512]{1,0:T(8,128)(2,1)S(1)}, bf16[256,512]{1,0:T(8,128)(2,1)S(1)}, u32[]{:S(2)}, u32[]{:S(2)}) collective-permute-start(bf16[256,512]{1,0:T(8,128)(2,1)S(1)} %get-tuple-element.19), channel_id=1, source_target_pairs={{0,1},{1,0},{2,3},{3,2},{4,5},{5,4},{6,7},{7,6},{8,9},{9,8},{10,11... | collective-permute-start | bytes 786440 | tf_op jit(solution)/shard_map/ppermute | solution.py:26
  29.8 9.0 %collective-permute-start.7 = (bf16[256,512]{1,0:T(8,128)(2,1)S(1)}, bf16[256,512]{1,0:T(8,128)(2,1)S(1)}, u32[]{:S(2)}, u32[]{:S(2)}) collective-permute-start(bf16[256,512]{1,0:T(8,128)(2,1)S(1)} %add_convert_fusion), channel_id=1, source_target_pairs={{0,2},{1,3},{2,0},{3,1},{4,6},{5,7},{6,4},{7,5},{8,10},{9,11},{10,... | collective-permute-start | bytes 786440 | tf_op jit(solution)/shard_map/ppermute | solution.py:392
  39.1 7.8 %collective-permute-start.9 = (bf16[256,512]{1,0:T(8,128)(2,1)S(1)}, bf16[256,512]{1,0:T(8,128)(2,1)S(1)}, u32[]{:S(2)}, u32[]{:S(2)}) collective-permute-start(bf16[256,512]{1,0:T(8,128)(2,1)S(1)} %fusion.2.mine), channel_id=1, source_target_pairs={{0,4},{4,0},{8,12},{12,8},{16,20},{20,16},{24,28},{28,24},{1,5},{5... | collective-permute-start | bytes 786440 | tf_op jit(solution)/shard_map/ppermute | solution.py:31
  46.9 6.9 %collective-permute-start.10 = (bf16[256,512]{1,0:T(8,128)(2,1)S(1)}, bf16[256,512]{1,0:T(8,128)(2,1)S(1)}, u32[]{:S(2)}, u32[]{:S(2)}) collective-permute-start(bf16[256,512]{1,0:T(8,128)(2,1)S(1)} %collective-permute-done.9.mine), channel_id=1, source_target_pairs={{0,8},{8,16},{12,4},{16,24},{20,12},{28,20},{4,0},{24,28},{1,9},{9... | collective-permute-start | bytes 786440 | tf_op jit(solution)/shard_map/ppermute | solution.py:40
  48.3 5.5 %collective-permute-start.8 = (bf16[256,512]{1,0:T(8,128)(2,1)S(1)}, bf16[256,512]{1,0:T(8,128)(2,1)S(1)}, u32[]{:S(2)}, u32[]{:S(2)}) collective-permute-start(bf16[256,512]{1,0:T(8,128)(2,1)S(1)} %fusion.2.mine), channel_id=1, source_target_pairs={{0,1},{1,0},{2,3},{3,2},{4,5},{5,4},{6,7},{7,6},{8,9},{9,8},{10,11... | collective-permute-start | bytes 786440 | tf_op jit(solution)/shard_map/ppermute | solution.py:26
  48.3 10.4 %collective-permute-start.12 = (bf16[256,512]{1,0:T(8,128)(2,1)S(1)}, bf16[256,512]{1,0:T(8,128)(2,1)S(1)}, u32[]{:S(2)}, u32[]{:S(2)}) collective-permute-start(bf16[256,512]{1,0:T(8,128)(2,1)S(1)} %collective-permute-done.9.mine), channel_id=1, source_target_pairs={{0,1},{1,0},{2,3},{3,2},{4,5},{5,4},{6,7},{7,6},{8,9},{9,8},{10,11... | collective-permute-start | bytes 786440 | tf_op jit(solution)/shard_map/ppermute | solution.py:26
  53.8 7.2 %collective-permute-start.11 = (bf16[256,512]{1,0:T(8,128)(2,1)S(1)}, bf16[256,512]{1,0:T(8,128)(2,1)S(1)}, u32[]{:S(2)}, u32[]{:S(2)}) collective-permute-start(bf16[256,512]{1,0:T(8,128)(2,1)S(1)} %collective-permute-done.10.mine), channel_id=1, source_target_pairs={{0,1},{1,0},{2,3},{3,2},{4,5},{5,4},{6,7},{7,6},{8,9},{9,8},{10,11... | collective-permute-start | bytes 786440 | tf_op jit(solution)/shard_map/ppermute | solution.py:26

commit v4 on v3

--- a/solution.py
+++ b/solution.py
@@ -1,5 +1,3 @@
-import functools
-
 import jax
 import jax.numpy as jnp
 from jax import lax
@@ -19,6 +17,10 @@
 
 def held(x):
     return pltpu.with_memory_space_constraint(x, pltpu.VMEM)
+
+
+def in_hbm(x):
+    return pltpu.with_memory_space_constraint(x, pltpu.HBM)
 
 
 def swap_core(x):
@@ -103,6 +105,35 @@
     by_twos(0, count, step)
 
 
+def loader(left_in, right_in, left, right, order, left_sem, right_sem):
+    def loads(channel):
+        return (
+            pltpu.make_async_copy(left_in.at[channel, 0], left.at[channel], left_sem.at[channel]),
+            pltpu.make_async_copy(right_in.at[channel, 0], right.at[channel], right_sem.at[channel]),
+        )
+
+    def fetch(first, count):
+        def body(i, carry):
+            for copy in loads(order[i]):
+                copy.start()
+            return carry
+
+        lax.fori_loop(first, count, body, 0)
+
+    def ready(channel):
+        for copy in loads(channel):
+            copy.wait()
+
+    def rest(first, count):
+        def body(i, carry):
+            ready(order[i])
+            return carry
+
+        lax.fori_loop(first, count, body, 0)
+
+    return fetch, ready, rest
+
+
 def own_sum_kernel(
     shifts_in, widths_in, state_in, left_in, right_in, acc, left, right, shifts,
     src, widths, order, small_sem, left_sem, right_sem
@@ -114,24 +145,11 @@
     ]
     for copy in small:
         copy.start()
-
-    def loads(channel):
-        return (
-            pltpu.make_async_copy(left_in.at[channel, 0], left.at[channel], left_sem.at[channel]),
-            pltpu.make_async_copy(right_in.at[channel, 0], right.at[channel], right_sem.at[channel]),
-        )
-
+    fetch, ready, rest = loader(left_in, right_in, left, right, order, left_sem, right_sem)
     small[0].wait()
     owned = list_channels(shifts, order, OWN)
     near = list_channels(shifts, order, NEAR, owned)
-    list_channels(shifts, order, FAR, near)
-
-    def fetch(i, carry):
-        for copy in loads(order[i]):
-            copy.start()
-        return carry
-
-    lax.fori_loop(0, left.shape[0], fetch, 0)
+    fetch(0, near)
     acc[...] = jnp.zeros_like(acc)
     small[1].wait()
     small[2].wait()
@@ -139,34 +157,33 @@
     cols = lax.broadcasted_iota(jnp.int32, src.shape, 1)
     inside = (rows < widths[0]) & (cols < widths[0])
     src[...] = jnp.where(inside, src[...], jnp.zeros_like(src))
-
-    def ready(channel):
-        for copy in loads(channel):
-            copy.wait()
-
     add_terms(owned, order, src, left, right, acc, ready)
-
-    def rest(i, carry):
-        ready(order[i])
-        return carry
-
-    lax.fori_loop(owned, left.shape[0], rest, 0)
-
-
-def next_sum_kernel(wanted, last, shifts, mine, other, acc_in, left, right, *rest):
-    if last:
-        keep, give, acc, src, order = rest
-    else:
-        acc, src, order = rest
-    count = list_channels(shifts, order, wanted)
-    join(src, mine, other, far_exists() if last else None)
+    rest(owned, near)
+
+
+def near_sum_kernel(
+    shifts, mine, other, acc_in, left_old, right_old, left_in, right_in, acc, left, right,
+    src, order, ahead, left_sem, right_sem
+):
+    far = list_channels(shifts, ahead, FAR)
+    fetch, _, rest = loader(left_in, right_in, left, right, ahead, left_sem, right_sem)
+    fetch(0, far)
+    count = list_channels(shifts, order, NEAR)
+    join(src, mine, other)
     acc[...] = acc_in[...]
     add_terms(count, order, src, left, right, acc, lambda channel: None)
-    if last:
-        half = keep.shape[0]
-        parity = lax.rem(lax.axis_index("chan"), 2)
-        keep[...] = acc[pl.ds(pl.multiple_of(parity * half, half), half), :]
-        give[...] = acc[pl.ds(pl.multiple_of((1 - parity) * half, half), half), :].astype(BF16)
+    rest(0, far)
+
+
+def far_sum_kernel(shifts, mine, other, acc_in, left, right, keep, give, acc, src, order):
+    count = list_channels(shifts, order, FAR)
+    join(src, mine, other, far_exists())
+    acc[...] = acc_in[...]
+    add_terms(count, order, src, left, right, acc, lambda channel: None)
+    half = keep.shape[0]
+    parity = lax.rem(lax.axis_index("chan"), 2)
+    keep[...] = acc[pl.ds(pl.multiple_of(parity * half, half), half), :]
+    give[...] = acc[pl.ds(pl.multiple_of((1 - parity) * half, half), half), :].astype(BF16)
 
 
 def cost(matmuls, pad):
@@ -199,30 +216,54 @@
         compiler_params=pltpu.CompilerParams(vmem_limit_bytes=ROOM),
         cost_estimate=cost(2 * chans / 3, pad),
         name="own_sum",
-    )(shifts, widths, *[pltpu.with_memory_space_constraint(x, pltpu.HBM) for x in (state, left, right)])
-
-
-def next_sum(wanted, last, shifts, mine, other, acc, left, right):
+    )(in_hbm(shifts), widths, *[in_hbm(x) for x in (state, left, right)])
+
+
+def near_sum(shifts, mine, other, acc, left, right, left_in, right_in):
+    chans, pad, _ = left.shape
+    blocks = jax.ShapeDtypeStruct((chans, pad, pad), BF16)
+    return pl.pallas_call(
+        near_sum_kernel,
+        in_specs=[SMEM] + [VMEM] * 5 + [ANY] * 2,
+        out_specs=[VMEM] * 3,
+        out_shape=[jax.ShapeDtypeStruct((pad, pad), F32), blocks, blocks],
+        scratch_shapes=[
+            pltpu.VMEM((pad, pad), BF16),
+            pltpu.SMEM((chans + 1,), jnp.int32),
+            pltpu.SMEM((chans + 1,), jnp.int32),
+            pltpu.SemaphoreType.DMA((chans,)),
+            pltpu.SemaphoreType.DMA((chans,)),
+        ],
+        input_output_aliases={4: 1, 5: 2},
+        compiler_params=pltpu.CompilerParams(vmem_limit_bytes=ROOM),
+        cost_estimate=cost(2 * chans / 3, pad),
+        name="near_sum",
+    )(
+        shifts,
+        *[held(x) for x in (mine, other, acc, left, right)],
+        *[in_hbm(x) for x in (left_in, right_in)],
+    )
+
+
+def far_sum(shifts, mine, other, acc, left, right):
     chans, pad, _ = left.shape
     half = pad // 2
-    whole = jax.ShapeDtypeStruct((pad, pad), F32)
-    scratch = [pltpu.VMEM((pad, pad), BF16), pltpu.SMEM((chans + 1,), jnp.int32)]
-    if last:
-        scratch = [pltpu.VMEM((pad, pad), F32)] + scratch
-    return pl.pallas_call(
-        functools.partial(next_sum_kernel, wanted, last),
+    return pl.pallas_call(
+        far_sum_kernel,
         in_specs=[SMEM] + [VMEM] * 5,
-        out_specs=[VMEM, VMEM] if last else VMEM,
+        out_specs=[VMEM] * 2,
         out_shape=[
             jax.ShapeDtypeStruct((half, pad), F32),
             jax.ShapeDtypeStruct((half, pad), BF16),
-        ]
-        if last
-        else whole,
-        scratch_shapes=scratch,
+        ],
+        scratch_shapes=[
+            pltpu.VMEM((pad, pad), F32),
+            pltpu.VMEM((pad, pad), BF16),
+            pltpu.SMEM((chans + 1,), jnp.int32),
+        ],
         compiler_params=pltpu.CompilerParams(vmem_limit_bytes=ROOM),
         cost_estimate=cost(2 * chans / 3, pad),
-        name="far_sum" if last else "near_sum",
+        name="far_sum",
     )(shifts, *[held(x) for x in (mine, other, acc, left, right)])
 
 
@@ -383,8 +424,8 @@
 
     near_m, near_o, far_m, far_o = exchange(state_m, 2)
     acc, left, right, shifts = own_sum(shifts, widths, state_blocks, left_blocks, right_blocks)
-    acc = next_sum(NEAR, False, shifts, near_m, near_o, acc, left, right)
-    keep, give = next_sum(FAR, True, shifts, far_m, far_o, acc, left, right)
+    acc, left, right = near_sum(shifts, near_m, near_o, acc, left, right, left_blocks, right_blocks)
+    keep, give = far_sum(shifts, far_m, far_o, acc, left, right)
 
     pair_sum = (keep + swap_core(give).astype(F32)).astype(BF16)
     total = pair_sum.astype(F32)

time: 63.9 us -> 64.9 us (1.016)
  Pallas kernels: 19.4 us -> 20.7 us
  waiting for transfers between devices: 27.4 us -> 28.5 us
  local copies, waits for them, and re-layouts: 0.72 us -> 0.07 us
    pallas_call x2, Pallas kernels: 4.13 us -> 5.31 us  [the longest x1 2.75 us: far_sum(): pl.pallas_call(far_sum_kernel, in_specs=[SMEM] + [VMEM] * 5, out_specs=[V...]
    ppermute x1, starting transfers between devices: 2.37 us -> 1.28 us  [body(): lax.ppermute(pair_sum, 'chan', [(i, (i + turn) % chan_count) for i in ran...]
    ppermute x3, starting transfers between devices: 4.52 us -> 5.3 us  [swap_near(): lax.ppermute(x, 'sec', [(i, i ^ 1) for i in range(count) if i ^ 1 < count])]
    unnamed x6 -> x4, local copies, waits for them, and re-layouts: 0.68 us -> 0.03 us
  transfers between devices with their start and end apart: 13 -> 13, of which waited for: 8 -> 8; matrix products, arithmetic and copies ran while one was open for 0% -> 0% of each run, Pallas kernels for 22% -> 24%
where the time goes in v4:
time: 64.9 us; the launch traced here: 64.7 us
  waiting for transfers between devices  28.5 us (44%)
  Pallas kernels  20.7 us (32%)
  starting transfers between devices  12 us (18%)
  between operations  2.12 us (3%)
  other arithmetic  1.42 us (2%)
    ppermute x3, waiting for transfers between devices, swap_near(): lax.ppermute(x, 'sec', [(i, i ^ 1) for i in range(count) if i ^ 1 < count])  11.2 us
    ppermute x3, waiting for transfers between devices, pass_far(): return lax.ppermute(x, 'sec', pairs + list(zip(sources, targets)))  9.23 us
    ppermute x1, waiting for transfers between devices, body(): lax.ppermute(pair_sum, 'chan', [(i, (i + turn) % chan_count) for i in ran...  6.48 us
    pallas_call x1, Pallas kernels, own_sum(): pl.pallas_call(own_sum_kernel, in_specs=[ANY] * 5, out_specs=[VMEM] * 3 +...  5.57 us
    ppermute x3, starting transfers between devices, swap_near(): lax.ppermute(x, 'sec', [(i, i ^ 1) for i in range(count) if i ^ 1 < count])  5.3 us
    pallas_call x1, Pallas kernels, own_turn(): pl.pallas_call(own_turn_kernel, in_specs=[SMEM, VMEM, VMEM, VMEM], out_sp...  4.81 us
    ppermute x3, starting transfers between devices, pass_far(): return lax.ppermute(x, 'sec', pairs + list(zip(sources, targets)))  4.66 us
    pallas_call x1, Pallas kernels, far_sum(): pl.pallas_call(far_sum_kernel, in_specs=[SMEM] + [VMEM] * 5, out_specs=[V...  2.75 us
  transfers between devices with their start and end apart: 13, of which 8 were waited for; matrix products, arithmetic and copies ran while one was open for 0% of the time, Pallas kernels for 24%

profile of v4, /device:TPU:0, one launch (start us, length us, event | category | flops | bytes accessed | tf_op | source)
XLA Modules:
  0.0 64.7 jit_solution(17132594106797595364)
XLA Ops:
  1.3 1.1 %and_select_fusion.2 = bf16[256,512]{1,0:T(8,128)(2,1)S(1)} fusion(bf16[1,512,512]{2,1,0:T(8,128)(2,1)} %state_in.1, s32[]{:T(128)S(6)} %select_n.22, pred[512]{0:T(512)(128)(4,1)S(1)} %iota_compare_fusion, pred[256]{0:T(512)(128)(4,1)S(1)} %add_compare_fusion), kind=kLoop, calls=%fused_computation.2 | loop fusion | flops 262144 | bytes 525060 | tf_op jit(solution)/shard_map/jit(_where)/select_n | solution.py:423
  2.5 3.0 %collective-permute-start = (bf16[128,512]{1,0:T(8,128)(2,1)S(1)}, bf16[128,512]{1,0:T(8,128)(2,1)S(1)}, u32[]{:S(2)}, u32[]{:S(2)}) collective-permute-start(bf16[128,512]{1,0:T(8,128)(2,1)S(1)} %get-tuple-element.33), channel_id=1, source_target_pairs={{0,4},{4,0},{8,12},{12,8},{16,20},{20,16},{24,28},{28,24},{1,5},{5... | collective-permute-start | bytes 393224 | tf_op jit(solution)/shard_map/ppermute | solution.py:33
  5.5 0.1 collective-permute-start.2
  5.6 4.3 %collective-permute-done = bf16[128,512]{1,0:T(8,128)(2,1)S(1)} collective-permute-done((bf16[128,512]{1,0:T(8,128)(2,1)S(1)}, bf16[128,512]{1,0:T(8,128)(2,1)S(1)}, u32[]{:S(2)}, u32[]{:S(2)}) %collective-permute-start) | collective-permute-done | bytes 131104 | tf_op jit(solution)/shard_map/ppermute | solution.py:33
  9.8 2.1 %collective-permute-start.1 = (bf16[128,512]{1,0:T(8,128)(2,1)S(1)}, bf16[128,512]{1,0:T(8,128)(2,1)S(1)}, u32[]{:S(2)}, u32[]{:S(2)}) collective-permute-start(bf16[128,512]{1,0:T(8,128)(2,1)S(1)} %collective-permute-done), channel_id=1, source_target_pairs={{0,8},{8,16},{12,4},{16,24},{20,12},{28,20},{4,0},{24,28},{1,9},{9... | collective-permute-start | bytes 393224 | tf_op jit(solution)/shard_map/ppermute | solution.py:42
  12.0 0.7 %collective-permute-done.2 = bf16[128,512]{1,0:T(8,128)(2,1)S(1)} collective-permute-done((bf16[128,512]{1,0:T(8,128)(2,1)S(1)}, bf16[128,512]{1,0:T(8,128)(2,1)S(1)}, u32[]{:S(2)}, u32[]{:S(2)}) %collective-permute-start.2) | collective-permute-done | bytes 131104 | tf_op jit(solution)/shard_map/ppermute | solution.py:33
  12.7 1.0 %collective-permute-start.3 = (bf16[128,512]{1,0:T(8,128)(2,1)S(1)}, bf16[128,512]{1,0:T(8,128)(2,1)S(1)}, u32[]{:S(2)}, u32[]{:S(2)}) collective-permute-start(bf16[128,512]{1,0:T(8,128)(2,1)S(1)} %collective-permute-done.2), channel_id=1, source_target_pairs={{0,8},{8,16},{12,4},{16,24},{20,12},{28,20},{4,0},{24,28},{1,9},{9... | collective-permute-start | bytes 393224 | tf_op jit(solution)/shard_map/ppermute | solution.py:42
  13.6 0.1 collective-permute-start.5
  13.7 2.2 %collective-permute-done.1 = bf16[128,512]{1,0:T(8,128)(2,1)S(1)} collective-permute-done((bf16[128,512]{1,0:T(8,128)(2,1)S(1)}, bf16[128,512]{1,0:T(8,128)(2,1)S(1)}, u32[]{:S(2)}, u32[]{:S(2)}) %collective-permute-start.1) | collective-permute-done | bytes 131104 | tf_op jit(solution)/shard_map/ppermute | solution.py:42
  16.0 1.6 %collective-permute-done.3 = bf16[128,512]{1,0:T(8,128)(2,1)S(1)} collective-permute-done((bf16[128,512]{1,0:T(8,128)(2,1)S(1)}, bf16[128,512]{1,0:T(8,128)(2,1)S(1)}, u32[]{:S(2)}, u32[]{:S(2)}) %collective-permute-start.3) | collective-permute-done | bytes 131104 | tf_op jit(solution)/shard_map/ppermute | solution.py:42
  17.6 0.1 collective-permute-start.4
  17.7 5.6 %own_sum.1 = (f32[512,512]{1,0:T(8,128)S(1)}, bf16[8,512,512]{2,1,0:T(8,128)(2,1)S(1)}, bf16[8,512,512]{2,1,0:T(8,128)(2,1)S(1)}, s32[8]{0:T(128)S(1)}) custom-call(s32[8]{0:T(128)} %shifts_in.1, s32[1]{0:T(128)} %copy.18.widths_in, bf16[1,512,512]{2,1,0:T(8,128)(2,1)} %state_in.1, bf16[8,1,512,512]{3,2,1,0:T(8,128)(2,1)} %left_in.3, ...), custom_call_target="tpu_custom_call" | custom-call | flops 1431655808 | bytes 2796202 | tf_op jit(solution)/shard_map/own_sum/pallas_call | solution.py:198
  23.3 0.0 collective-permute-done.5.other
  23.3 2.6 %near_sum.1 = (f32[512,512]{1,0:T(8,128)S(1)}, bf16[8,512,512]{2,1,0:T(8,128)(2,1)S(1)}, bf16[8,512,512]{2,1,0:T(8,128)(2,1)S(1)}) custom-call(s32[8]{0:T(128)S(1)} %get-tuple-element.17.shifts, bf16[256,512]{1,0:T(8,128)(2,1)S(1)} %constant_dynamic-update-slice_fusion.2.mine, ...), custom_call_target="tpu_custom_call", output_to_operand_aliasing={{1}: (4, {}), {2}: (5, {})} | custom-call | flops 1431655808 | bytes 2796202 | tf_op jit(solution)/shard_map/near_sum/pallas_call | solution.py:225
  25.9 0.0 copy-start
  25.9 2.7 %far_sum.1 = (f32[256,512]{1,0:T(8,128)S(1)}, bf16[256,512]{1,0:T(8,128)(2,1)S(1)}) custom-call(s32[8]{0:T(128)S(1)} %get-tuple-element.17.shifts, bf16[256,512]{1,0:T(8,128)(2,1)S(1)} %constant_dynamic-update-slice_fusion.mine, bf16[256,512]{1,0:T(8,128)(2,1)S(1)} %collective-permute-done.4.other, f32[512,512]{1,0:T(8,128)S(1)} %get-tuple-element.21.acc_in, ...), custom_call_target="tpu_custom_call" | custom-call | flops 1431655808 | bytes 2796202 | tf_op jit(solution)/shard_map/far_sum/pallas_call | solution.py:251
  28.6 0.1 collective-permute-start.6
  28.7 1.5 %collective-permute-done.6 = bf16[256,512]{1,0:T(8,128)(2,1)S(1)} collective-permute-done((bf16[256,512]{1,0:T(8,128)(2,1)S(1)}, bf16[256,512]{1,0:T(8,128)(2,1)S(1)}, u32[]{:S(2)}, u32[]{:S(2)}) %collective-permute-start.6) | collective-permute-done | bytes 262176 | tf_op jit(solution)/shard_map/ppermute | solution.py:28
  30.2 0.1 add_convert_fusion
  30.3 1.3 %collective-permute-start.7 = (bf16[256,512]{1,0:T(8,128)(2,1)S(1)}, bf16[256,512]{1,0:T(8,128)(2,1)S(1)}, u32[]{:S(2)}, u32[]{:S(2)}) collective-permute-start(bf16[256,512]{1,0:T(8,128)(2,1)S(1)} %add_convert_fusion), channel_id=1, source_target_pairs={{0,2},{1,3},{2,0},{3,1},{4,6},{5,7},{6,4},{7,5},{8,10},{9,11},{10,... | collective-permute-start | bytes 786440 | tf_op jit(solution)/shard_map/ppermute | solution.py:433
  32.3 6.5 %collective-permute-done.7 = bf16[256,512]{1,0:T(8,128)(2,1)S(1)} collective-permute-done((bf16[256,512]{1,0:T(8,128)(2,1)S(1)}, bf16[256,512]{1,0:T(8,128)(2,1)S(1)}, u32[]{:S(2)}, u32[]{:S(2)}) %collective-permute-start.7) | collective-permute-done | bytes 262176 | tf_op jit(solution)/shard_map/ppermute | solution.py:433
  38.7 0.2 fusion.2.mine
  39.0 2.2 %collective-permute-start.9 = (bf16[256,512]{1,0:T(8,128)(2,1)S(1)}, bf16[256,512]{1,0:T(8,128)(2,1)S(1)}, u32[]{:S(2)}, u32[]{:S(2)}) collective-permute-start(bf16[256,512]{1,0:T(8,128)(2,1)S(1)} %fusion.2.mine), channel_id=1, source_target_pairs={{0,4},{4,0},{8,12},{12,8},{16,20},{20,16},{24,28},{28,24},{1,5},{5... | collective-permute-start | bytes 786440 | tf_op jit(solution)/shard_map/ppermute | solution.py:33
  41.2 6.3 %collective-permute-done.9.mine = bf16[256,512]{1,0:T(8,128)(2,1)S(1)} collective-permute-done((bf16[256,512]{1,0:T(8,128)(2,1)S(1)}, bf16[256,512]{1,0:T(8,128)(2,1)S(1)}, u32[]{:S(2)}, u32[]{:S(2)}) %collective-permute-start.9) | collective-permute-done | bytes 262176 | tf_op jit(solution)/shard_map/ppermute | solution.py:33
  47.4 1.6 %collective-permute-start.10 = (bf16[256,512]{1,0:T(8,128)(2,1)S(1)}, bf16[256,512]{1,0:T(8,128)(2,1)S(1)}, u32[]{:S(2)}, u32[]{:S(2)}) collective-permute-start(bf16[256,512]{1,0:T(8,128)(2,1)S(1)} %collective-permute-done.9.mine), channel_id=1, source_target_pairs={{0,8},{8,16},{12,4},{16,24},{20,12},{28,20},{4,0},{24,28},{1,9},{9... | collective-permute-start | bytes 786440 | tf_op jit(solution)/shard_map/ppermute | solution.py:42
  49.0 0.0 collective-permute-start.8
  49.0 0.5 collective-permute-start.12
  49.5 5.3 %collective-permute-done.10.mine = bf16[256,512]{1,0:T(8,128)(2,1)S(1)} collective-permute-done((bf16[256,512]{1,0:T(8,128)(2,1)S(1)}, bf16[256,512]{1,0:T(8,128)(2,1)S(1)}, u32[]{:S(2)}, u32[]{:S(2)}) %collective-permute-start.10) | collective-permute-done | bytes 262176 | tf_op jit(solution)/shard_map/ppermute | solution.py:42
  54.9 4.8 %own_turn.1 = (bf16[128,512]{1,0:T(8,128)(2,1)}, bf16[8,1,512,512]{3,2,1,0:T(8,128)(2,1)}, bf16[8,512,512]{2,1,0:T(8,128)(2,1)S(1)}, bf16[512,512]{1,0:T(8,128)(2,1)S(1)}) custom-call(s32[8]{0:T(128)S(1)} %get-tuple-element.17.shifts, bf16[256,512]{1,0:T(8,128)(2,1)S(1)} %fusion.2.mine, bf16[256,512]{1,0:T(8,128)(2,1)S(1)} %collective-permute-done.8.other, ...), custom_call_target="tpu_custom_call" | custom-call | flops 2147483648 | bytes 4194304 | tf_op jit(solution)/shard_map/own_turn/pallas_call | solution.py:334
  59.7 0.0 collective-permute-done.12.other
  59.7 2.3 %near_turn.1 = (bf16[8,1,512,512]{3,2,1,0:T(8,128)(2,1)}, bf16[8,512,512]{2,1,0:T(8,128)(2,1)S(1)}) custom-call(s32[8]{0:T(128)S(1)} %get-tuple-element.17.shifts, bf16[256,512]{1,0:T(8,128)(2,1)S(1)} %collective-permute-done.9.mine, bf16[256,512]{1,0:T(8,128)(2,1)S(1)} %collective-permute-done.12.other, ...), custom_call_target="tpu_custom_call", output_to_operand_aliasing={{0}: (6, {})} | custom-call | flops 1431655808 | bytes 2796202 | tf_op jit(solution)/shard_map/near_turn/pallas_call | solution.py:363
  62.0 2.7 %far_turn.1 = bf16[8,1,512,512]{3,2,1,0:T(8,128)(2,1)} custom-call(s32[8]{0:T(128)S(1)} %get-tuple-element.17.shifts, bf16[256,512]{1,0:T(8,128)(2,1)S(1)} %collective-permute-done.10.mine, bf16[256,512]{1,0:T(8,128)(2,1)S(1)} %collective-permute-done.11.other, ...), custom_call_target="tpu_custom_call", output_to_operand_aliasing={{}: (4, {})} | custom-call | flops 715827904 | bytes 1398101 | tf_op jit(solution)/shard_map/far_turn/pallas_call | solution.py:387
  (13 shorter events, 0.1 us)
Async XLA Ops:
  2.5 7.4 %collective-permute-start = (bf16[128,512]{1,0:T(8,128)(2,1)S(1)}, bf16[128,512]{1,0:T(8,128)(2,1)S(1)}, u32[]{:S(2)}, u32[]{:S(2)}) collective-permute-start(bf16[128,512]{1,0:T(8,128)(2,1)S(1)} %get-tuple-element.33), channel_id=1, source_target_pairs={{0,4},{4,0},{8,12},{12,8},{16,20},{20,16},{24,28},{28,24},{1,5},{5... | collective-permute-start | bytes 393224 | tf_op jit(solution)/shard_map/ppermute | solution.py:33
  5.5 7.2 %collective-permute-start.2 = (bf16[128,512]{1,0:T(8,128)(2,1)S(1)}, bf16[128,512]{1,0:T(8,128)(2,1)S(1)}, u32[]{:S(2)}, u32[]{:S(2)}) collective-permute-start(bf16[128,512]{1,0:T(8,128)(2,1)S(1)} %get-tuple-element.32), channel_id=1, source_target_pairs={{0,4},{4,0},{8,12},{12,8},{16,20},{20,16},{24,28},{28,24},{1,5},{5... | collective-permute-start | bytes 393224 | tf_op jit(solution)/shard_map/ppermute | solution.py:33
  9.8 6.1 %collective-permute-start.1 = (bf16[128,512]{1,0:T(8,128)(2,1)S(1)}, bf16[128,512]{1,0:T(8,128)(2,1)S(1)}, u32[]{:S(2)}, u32[]{:S(2)}) collective-permute-start(bf16[128,512]{1,0:T(8,128)(2,1)S(1)} %collective-permute-done), channel_id=1, source_target_pairs={{0,8},{8,16},{12,4},{16,24},{20,12},{28,20},{4,0},{24,28},{1,9},{9... | collective-permute-start | bytes 393224 | tf_op jit(solution)/shard_map/ppermute | solution.py:42
  12.7 5.0 %collective-permute-start.3 = (bf16[128,512]{1,0:T(8,128)(2,1)S(1)}, bf16[128,512]{1,0:T(8,128)(2,1)S(1)}, u32[]{:S(2)}, u32[]{:S(2)}) collective-permute-start(bf16[128,512]{1,0:T(8,128)(2,1)S(1)} %collective-permute-done.2), channel_id=1, source_target_pairs={{0,8},{8,16},{12,4},{16,24},{20,12},{28,20},{4,0},{24,28},{1,9},{9... | collective-permute-start | bytes 393224 | tf_op jit(solution)/shard_map/ppermute | solution.py:42
  13.6 9.6 %collective-permute-start.5 = (bf16[256,512]{1,0:T(8,128)(2,1)S(1)}, bf16[256,512]{1,0:T(8,128)(2,1)S(1)}, u32[]{:S(2)}, u32[]{:S(2)}) collective-permute-start(bf16[256,512]{1,0:T(8,128)(2,1)S(1)} %constant_dynamic-update-slice_fusion.2.mine), channel_id=1, source_target_pairs={{0,1},{1,0},{2,3},{3,2},{4,5},{5,4},{6,7},{7,6},{8,9},{9,8},{10,11... | collective-permute-start | bytes 786440 | tf_op jit(solution)/shard_map/ppermute | solution.py:28
  17.6 8.2 %collective-permute-start.4 = (bf16[256,512]{1,0:T(8,128)(2,1)S(1)}, bf16[256,512]{1,0:T(8,128)(2,1)S(1)}, u32[]{:S(2)}, u32[]{:S(2)}) collective-permute-start(bf16[256,512]{1,0:T(8,128)(2,1)S(1)} %constant_dynamic-update-slice_fusion.mine), channel_id=1, source_target_pairs={{0,1},{1,0},{2,3},{3,2},{4,5},{5,4},{6,7},{7,6},{8,9},{9,8},{10,11... | collective-permute-start | bytes 786440 | tf_op jit(solution)/shard_map/ppermute | solution.py:28
  25.9 12.9 %copy-start = (bf16[1,512,512]{2,1,0:T(8,128)(2,1)S(1)}, bf16[1,512,512]{2,1,0:T(8,128)(2,1)}, u32[]{:S(2)}) copy-start(bf16[1,512,512]{2,1,0:T(8,128)(2,1)} %state_in.1) | copy-start | bytes 1572868
  28.6 1.6 %collective-permute-start.6 = (bf16[256,512]{1,0:T(8,128)(2,1)S(1)}, bf16[256,512]{1,0:T(8,128)(2,1)S(1)}, u32[]{:S(2)}, u32[]{:S(2)}) collective-permute-start(bf16[256,512]{1,0:T(8,128)(2,1)S(1)} %get-tuple-element.25), channel_id=1, source_target_pairs={{0,1},{1,0},{2,3},{3,2},{4,5},{5,4},{6,7},{7,6},{8,9},{9,8},{10,11... | collective-permute-start | bytes 786440 | tf_op jit(solution)/shard_map/ppermute | solution.py:28
  30.3 8.4 %collective-permute-start.7 = (bf16[256,512]{1,0:T(8,128)(2,1)S(1)}, bf16[256,512]{1,0:T(8,128)(2,1)S(1)}, u32[]{:S(2)}, u32[]{:S(2)}) collective-permute-start(bf16[256,512]{1,0:T(8,128)(2,1)S(1)} %add_convert_fusion), channel_id=1, source_target_pairs={{0,2},{1,3},{2,0},{3,1},{4,6},{5,7},{6,4},{7,5},{8,10},{9,11},{10,... | collective-permute-start | bytes 786440 | tf_op jit(solution)/shard_map/ppermute | solution.py:433
  39.0 8.5 %collective-permute-start.9 = (bf16[256,512]{1,0:T(8,128)(2,1)S(1)}, bf16[256,512]{1,0:T(8,128)(2,1)S(1)}, u32[]{:S(2)}, u32[]{:S(2)}) collective-permute-start(bf16[256,512]{1,0:T(8,128)(2,1)S(1)} %fusion.2.mine), channel_id=1, source_target_pairs={{0,4},{4,0},{8,12},{12,8},{16,20},{20,16},{24,28},{28,24},{1,5},{5... | collective-permute-start | bytes 786440 | tf_op jit(solution)/shard_map/ppermute | solution.py:33
  47.4 7.4 %collective-permute-start.10 = (bf16[256,512]{1,0:T(8,128)(2,1)S(1)}, bf16[256,512]{1,0:T(8,128)(2,1)S(1)}, u32[]{:S(2)}, u32[]{:S(2)}) collective-permute-start(bf16[256,512]{1,0:T(8,128)(2,1)S(1)} %collective-permute-done.9.mine), channel_id=1, source_target_pairs={{0,8},{8,16},{12,4},{16,24},{20,12},{28,20},{4,0},{24,28},{1,9},{9... | collective-permute-start | bytes 786440 | tf_op jit(solution)/shard_map/ppermute | solution.py:42
  49.0 5.9 %collective-permute-start.8 = (bf16[256,512]{1,0:T(8,128)(2,1)S(1)}, bf16[256,512]{1,0:T(8,128)(2,1)S(1)}, u32[]{:S(2)}, u32[]{:S(2)}) collective-permute-start(bf16[256,512]{1,0:T(8,128)(2,1)S(1)} %fusion.2.mine), channel_id=1, source_target_pairs={{0,1},{1,0},{2,3},{3,2},{4,5},{5,4},{6,7},{7,6},{8,9},{9,8},{10,11... | collective-permute-start | bytes 786440 | tf_op jit(solution)/shard_map/ppermute | solution.py:28
  49.0 10.7 %collective-permute-start.12 = (bf16[256,512]{1,0:T(8,128)(2,1)S(1)}, bf16[256,512]{1,0:T(8,128)(2,1)S(1)}, u32[]{:S(2)}, u32[]{:S(2)}) collective-permute-start(bf16[256,512]{1,0:T(8,128)(2,1)S(1)} %collective-permute-done.9.mine), channel_id=1, source_target_pairs={{0,1},{1,0},{2,3},{3,2},{4,5},{5,4},{6,7},{7,6},{8,9},{9,8},{10,11... | collective-permute-start | bytes 786440 | tf_op jit(solution)/shard_map/ppermute | solution.py:28
  54.9 7.2 %collective-permute-start.11 = (bf16[256,512]{1,0:T(8,128)(2,1)S(1)}, bf16[256,512]{1,0:T(8,128)(2,1)S(1)}, u32[]{:S(2)}, u32[]{:S(2)}) collective-permute-start(bf16[256,512]{1,0:T(8,128)(2,1)S(1)} %collective-permute-done.10.mine), channel_id=1, source_target_pairs={{0,1},{1,0},{2,3},{3,2},{4,5},{5,4},{6,7},{7,6},{8,9},{9,8},{10,11... | collective-permute-start | bytes 786440 | tf_op jit(solution)/shard_map/ppermute | solution.py:28
